TPU v7x, 32 devices: a whole 2x2x4 slice. The times are simulated.
32 devices in a mesh: gx: 4 (over y, core), gy: 8 (over z, x).
Axes of the slice: x: 2, y: 2, z: 4, core: 2. Of those that a mesh axis runs over, the one named last changes fastest.
Arguments:
- forcing: float32 [2, 20, 64, 1024], P(None, None, 'gx', 'gy'), may hold values from -6 to 6
- viscosity: float32 [20, 64, 1024], P(None, 'gx', 'gy'), may hold values from 0.5 to 8
- spread: float32 [20, 64, 1024], P(None, 'gx', 'gy'), may hold values from 0.2 to 2
- coupling: float32 [64, 1024], P('gx', 'gy'), may hold values from -0.5 to 0.5
- friction: float32 [64, 1024], P('gx', 'gy'), may hold values from 0.05 to 5
- ice_mask: int32 [64, 1024], P('gx', 'gy'), may hold values 0 or 1
- aggregates: int32 [64, 1024], P('gx', 'gy'), may hold values from 0 to 127, as said below
Outputs:
- solution: float32 [2, 20, 64, 1024], P(None, None, 'gx', 'gy')
- residual: float32 [2, 20, 64, 1024], P(None, None, 'gx', 'gy')
Inputs may be any that keep to these rules, and one draw needn't show every extreme that they name: `aggregates`: within each device block of 16 x 128 columns, every number from 0 to 127 names some columns of that block.
All inputs are finite; a program needn't handle non-finite values. No bound on the sum of `ice_mask` on one device may be relied on, other than what follows from the above.
Results may differ from a plain program's by a relative error of at most 0.0013.
Values sent between devices are 32-bit elements; how exact they have to be, the bound alone decides.
A program may use at most 128 MiB of HBM per device.

v0:
```python
import jax
import jax.numpy as jnp
from jax import lax
from jax.experimental import pallas as pl
from jax.experimental.pallas import tpu as pltpu
from jax.sharding import PartitionSpec as P

ITERS = 3
CSWEEPS = 4
LINE_WEIGHT = 0.8
POINT_WEIGHT = 0.7
COARSE_WEIGHT = 0.7
MESH = pl.DeviceIdType.MESH
F32 = jnp.float32
BF16 = jnp.bfloat16
TOP = 8
HALO = 8
SLOT = 2 * HALO
STEPS = ((1, 0), (-1, 0), (0, 1), (0, -1), (1, 1), (1, -1), (-1, 1), (-1, -1))
BACK = (1, 0, 3, 2, 7, 6, 5, 4)


def split(x):
    high = x.astype(BF16)
    return high, (x - high.astype(F32)).astype(BF16)


def dot(a, b, ca, cb):
    return lax.dot_general(a, b, (((ca,), (cb,)), ((), ())), preferred_element_type=F32)


def total(x):
    return jnp.sum(jnp.sum(x, axis=1, keepdims=True), axis=0, keepdims=True)


def turn(x, shift):
    flat = x.reshape(-1, x.shape[-1])
    return pltpu.roll(flat, shift % x.shape[-1], 1).reshape(x.shape)


def kernel(nx, ny, layers, cx, cy, forcing, viscosity, spread, coupling, friction, mask, aggs,
           solution, residual, *scratch):
    count = nx * ny
    gx = lax.axis_index("gx")
    gy = lax.axis_index("gy")
    me = gx * ny + gy
    (levels, (basis, stored, visc, spr, misc), (hit, big_hi, big_lo, point_diag, point_cross),
     (x_out, x_in, x_send, x_recv), gathers, first_swap, right_swap, side_swap, point_swap,
     (mid_rows, col_rows)) = scratch
    tall = cx + 2 * HALO
    own = pl.ds(HALO, cx)
    slots = cy // SLOT
    lane = lax.broadcasted_iota(jnp.int32, (cx, cy), 1)
    row = lax.broadcasted_iota(jnp.int32, (cx, cy), 0)
    first_lane, last_lane = lane == 0, lane == cy - 1
    long_lane = lax.broadcasted_iota(jnp.int32, (tall, cy), 1)
    kept_lane = (long_lane < HALO) | (long_lane >= cy - HALO)

    exists, peers = [], []
    for dx, dy in STEPS:
        ok = []
        if dx:
            ok.append(gx < nx - 1 if dx > 0 else gx > 0)
        if dy:
            ok.append(gy < ny - 1 if dy > 0 else gy > 0)
        exists.append(ok[0] if len(ok) == 1 else jnp.logical_and(ok[0], ok[1]))
        peers.append((gx + dx, gy + dy))

    class Swap:
        def __init__(self, pieces, send, recv):
            self.pieces = pieces
            self.copies = [[pltpu.make_async_remote_copy(
                src_ref=src, dst_ref=dst, send_sem=send.at[d, i], recv_sem=recv.at[BACK[d], i],
                device_id=peers[d], device_id_type=MESH) for i, (src, dst) in enumerate(pieces[d])]
                for d in range(len(pieces))]

        def start(self, which=None):
            for d in range(len(self.copies)) if which is None else which:
                @pl.when(exists[d])
                def _():
                    for copy in self.copies[d]:
                        copy.start()

        def wait(self):
            for d in range(len(self.copies)):
                @pl.when(exists[d])
                def _():
                    for copy in self.copies[d]:
                        copy.wait_send()
                    for copy in self.copies[BACK[d]]:
                        copy.wait_recv()

        def clear(self):
            for d in range(len(self.copies)):
                @pl.when(jnp.logical_not(exists[d]))
                def _():
                    for _, ref in self.pieces[BACK[d]]:
                        ref[...] = jnp.zeros(ref.shape, F32)

    def edges(rows, packed, landed):
        low, high = pl.ds(0, HALO), pl.ds(cx - HALO, HALO)
        top, bottom = pl.ds(0, HALO), pl.ds(HALO + cx, HALO)
        return [
            [(src(cx - HALO), dst(0)) for src, dst in rows],
            [(src(0), dst(1)) for src, dst in rows],
            [(packed, landed.at[0, :, own])],
            [(packed, landed.at[1, :, own])],
            [(packed.at[:, high], landed.at[0, :, top])],
            [(packed.at[:, high], landed.at[1, :, top])],
            [(packed.at[:, low], landed.at[0, :, bottom])],
            [(packed.at[:, low], landed.at[1, :, bottom])],
        ]

    def ends(e):
        return pl.ds(0, HALO) if e == 0 else pl.ds(HALO + cx, HALO)

    class Packer:
        def __init__(self, out):
            self.out = out
            self.at = 0
            self.tile = None

        def add(self, value):
            s, m = divmod(self.at, slots)
            moved = pltpu.roll(value, (SLOT * m + HALO) % cy, 1)
            self.tile = moved if m == 0 else jnp.where(lane // SLOT == m, moved, self.tile)
            self.at += 1
            if m == slots - 1:
                self.flush(s)

        def flush(self, s):
            self.out[s] = self.tile
            self.tile = None

        def finish(self):
            if self.tile is not None:
                self.flush((self.at - 1) // slots)

    def unpack(landed, puts):
        south = long_lane % SLOT < HALO
        comb = None
        for i, put in enumerate(puts):
            s, m = divmod(i, slots)
            if m == 0:
                comb = jnp.where(south, landed[0, s], landed[1, s])
            put(jnp.where(kept_lane, pltpu.roll(comb, (cy - SLOT * m - HALO) % cy, 1), 0.0))

    chunks = ((0, tall // 2), (tall // 2, tall // 2))
    both = (0, 1)

    class Level:
        def __init__(self, depth, refs):
            self.depth = depth
            (self.field, self.diag, self.vert, self.side, self.cross, self.inverse, self.upper,
             self.right, self.forward) = refs

        def at(self, p, k, t, c0, cn, shift=0):
            return self.field[p, k, t, :, pl.ds(TOP + c0 + shift, cn), :]

        def sideways(self, p, k, c0, cn, tiles):
            here = pl.ds(c0, cn)
            wide = lax.broadcasted_iota(jnp.int32, (2, cn, cy), 2)
            value = [self.at(p, k, t, c0, cn) for t in both]
            up = [turn(v, cy - 1) for v in value]
            down = [turn(v, 1) for v in value]
            outs = []
            for t in tiles:
                north = jnp.where(wide == cy - 1, up[1 - t], up[t])
                south = jnp.where(wide == 0, down[1 - t], down[t])
                out = (self.side[0, k, t, here][None] * self.at(p, k, t, c0, cn, 1)
                       + self.side[1, k, t, here][None] * self.at(p, k, t, c0, cn, -1)
                       + self.side[2, k, t, here][None] * north + self.side[3, k, t, here][None] * south)
                if k == 0:
                    crossed = self.cross[t, here]
                    out = out - jnp.stack([crossed * value[t][1], crossed * value[t][0]])
                outs.append(out)
            return value, outs

        def leftover(self, p, right, emit, tiles=both, spans=chunks):
            for c0, cn in spans:
                here = pl.ds(c0, cn)
                for k in range(self.depth):
                    value, outs = self.sideways(p, k, c0, cn, tiles)
                    for i, t in enumerate(tiles):
                        out = outs[i] - self.diag[k, t, here][None] * value[t]
                        if k + 1 < self.depth:
                            out = out + self.vert[k, t, here][None] * self.at(p, k + 1, t, c0, cn)
                        if k > 0:
                            out = out + self.vert[k - 1, t, here][None] * self.at(p, k - 1, t, c0, cn)
                        emit(k, t, c0, cn, right(k, t, here) + out)

        def solve(self, source, old, p):
            for c0, cn in chunks:
                here = pl.ds(c0, cn)
                last = [None, None]
                for k in range(self.depth):
                    values = source(k, c0, cn)
                    for t in both:
                        value = values[t]
                        if k > 0:
                            value = value + self.vert[k - 1, t, here][None] * last[t]
                        last[t] = value * self.inverse[k, t, here][None]
                        self.forward[k, t, :, here] = last[t]
                for k in reversed(range(self.depth)):
                    for t in both:
                        if k + 1 < self.depth:
                            last[t] = self.forward[k, t, :, here] - self.upper[k, t, here][None] * last[t]
                        value = LINE_WEIGHT * last[t]
                        if old is not None:
                            value = value + (1.0 - LINE_WEIGHT) * self.at(old, k, t, c0, cn)
                        self.field[p, k, t, :, pl.ds(TOP + c0, cn), :] = value

        def first(self, right):
            self.solve(lambda k, c0, cn: [right(k, t, pl.ds(c0, cn)) for t in both], None, 0)

        def sweep(self, p, right):
            def source(k, c0, cn):
                outs = self.sideways(p, k, c0, cn, both)[1]
                return [right(k, t, pl.ds(c0, cn)) + outs[t] for t in both]
            self.solve(source, p, 1 - p)

        def factor(self):
            inverse = 1.0 / self.diag[0]
            self.inverse[0] = inverse
            for k in range(1, self.depth):
                ratio = -self.vert[k - 1] * inverse
                self.upper[k - 1] = ratio
                inverse = 1.0 / (self.diag[k] + self.vert[k - 1] * ratio)
                self.inverse[k] = inverse

        def after(self, right):
            self.sweep(0, right)
            self.sweep(1, right)

    half = layers // 2
    fine, middle, column = (Level(n, refs) for n, refs in zip((layers, half, 1), levels))
    for level in (fine, middle, column):
        for p in range(2):
            for k in range(level.depth):
                for t in both:
                    level.field[p, k, t, :, pl.ds(0, TOP), :] = jnp.zeros((2, TOP, cy), F32)
                    level.field[p, k, t, :, pl.ds(TOP + tall, TOP), :] = jnp.zeros((2, TOP, cy), F32)

    def rows_of(ref, at):
        return lambda start: ref.at[at + (pl.ds(start, HALO),)]

    any_k = slice(None)

    (first_pack, first_land, first_send, first_recv) = first_swap
    swap0 = Swap(edges([
        (lambda lo: forcing.at[:, :, pl.ds(lo, HALO)], lambda e: basis.at[0, :, :, 0, ends(e)]),
        (lambda lo: viscosity.at[:, pl.ds(lo, HALO)], lambda e: visc.at[:, 0, ends(e)]),
        (lambda lo: spread.at[:, pl.ds(lo, HALO)], lambda e: spr.at[:, 0, ends(e)]),
        (lambda lo: misc.at[:, 0, pl.ds(HALO + lo, HALO)], lambda e: misc.at[:, 0, ends(e)]),
    ], first_pack, first_land), first_send, first_recv)
    (right_pack, right_land, right_send, right_recv) = right_swap

    def swap_right(j):
        return Swap(edges([(lambda lo: basis.at[j, :, :, 0, pl.ds(HALO + lo, HALO)],
                            lambda e: basis.at[j, :, :, 0, ends(e)])],
                          right_pack, right_land), right_send, right_recv)

    (side_pack, side_land, side_send, side_recv) = side_swap
    swap_side = Swap(edges([
        (lambda lo: middle.field.at[1, :, 0, :, pl.ds(TOP + HALO + lo, HALO)], lambda e: mid_rows.at[e]),
        (lambda lo: column.field.at[1, 0, 0, :, pl.ds(TOP + HALO + lo, HALO)], lambda e: col_rows.at[e, 0]),
        (lambda lo: column.right.at[0, 0, :, pl.ds(HALO + lo, HALO)], lambda e: col_rows.at[e, 1]),
    ], side_pack, side_land), side_send, side_recv)
    (far_out, far_in, far_send, far_recv) = point_swap
    swap_far = Swap([[(far_out, far_in.at[d])] for d in range(8)], far_send, far_recv)

    def near_swap(p, q):
        return Swap([[(x_out.at[p], x_in.at[q, d])] for d in range(4)], x_send.at[p], x_recv.at[q])

    misc[0, 0, own] = mask[...].astype(F32)
    misc[1, 0, own] = aggs[...].astype(F32)
    misc[2, 0, own] = friction[...]
    misc[3, 0, own] = coupling[...]
    swap0.start((0, 1))
    packer = Packer(first_pack)
    for i in range(4):
        packer.add(misc[i, 0, own])
    for k in range(layers):
        packer.add(viscosity[k])
        packer.add(spread[k])
    for k in range(layers):
        for v in range(2):
            packer.add(forcing[v, k])
    packer.finish()
    swap0.start(range(2, 8))
    for j in range(1, ITERS):
        swap_right(j).clear()
    swap0.clear()
    swap_side.clear()
    swap_far.clear()
    for q in range(2):
        near_swap(0, q).clear()
    for k in range(layers):
        visc[k, 0, own] = viscosity[k]
        spr[k, 0, own] = spread[k]
        basis[0, :, k, 0, own] = forcing[:, k]

    def gather(which, slot=0):
        out, into, send, recv = gathers[which]
        into, recv = into.at[slot], recv.at[slot]
        rest = into.at[pl.ds(0, count - 1)]

        def start():
            def step(i, carry):
                target = lax.rem(me + i, count)
                pltpu.make_async_remote_copy(
                    src_ref=out, dst_ref=into.at[me], send_sem=send, recv_sem=recv,
                    device_id=(target // ny, lax.rem(target, ny)), device_id_type=MESH).start()
                return carry

            lax.fori_loop(1, count, step, 0)
            into[me] = out[...]

        def wait():
            pltpu.make_async_copy(rest, rest, recv).wait()
            pltpu.make_async_copy(rest, rest, send).wait()

        return start, wait

    wide = lax.broadcasted_iota(jnp.int32, (1, cy), 1)

    def reduce_all(parts):
        line = jnp.zeros((1, cy), F32)
        for i, part in enumerate(parts):
            line = jnp.where(wide == i, part, line)
        gathers[1][0][...] = line
        start, wait = gather(1)
        start()
        wait()
        return jnp.sum(gathers[1][1][0, :, 0, :], axis=0, keepdims=True)

    def pick(line, i):
        return jnp.sum(jnp.where(wide == i, line, 0.0), axis=1, keepdims=True)

    def put_to(ref, *at):
        def put(value):
            ref[at] = value
        return put

    swap0.wait()
    puts = [put_to(misc, i, 1) for i in range(4)]
    for k in range(layers):
        puts += [put_to(visc, k, 1), put_to(spr, k, 1)]
    for k in range(layers):
        puts += [put_to(basis, 0, v, k, 1) for v in range(2)]
    unpack(first_land, puts)

    ids_all = [misc[1, t].astype(jnp.int32) for t in both]
    ids = misc[1, 0, own].astype(jnp.int32)
    ice = [misc[0, t] for t in both]
    for t in both:
        column.field[1, 0, t, 0, pl.ds(TOP, tall), :] = ice[t]
    around = []
    ups = [turn(x, cy - 1) for x in ice]
    downs = [turn(x, 1) for x in ice]
    for t in both:
        around.append((column.field[1, 0, t, 0, pl.ds(TOP + 1, tall), :],
                       column.field[1, 0, t, 0, pl.ds(TOP - 1, tall), :],
                       jnp.where(long_lane == cy - 1, ups[1 - t], ups[t]),
                       jnp.where(long_lane == 0, downs[1 - t], downs[t])))
    for k in range(layers):
        for t in both:
            owned = spr[k, t]
            faces = 4.0 * owned
            if k + 1 < layers:
                face = 0.5 * (visc[k, t] + visc[k + 1, t]) * ice[t]
                fine.vert[k, t] = face
                faces = faces + face
            if k > 0:
                faces = faces + fine.vert[k - 1, t]
            if k == 0:
                faces = faces + misc[2, t]
            fine.diag[k, t] = ice[t] * faces + (1.0 - ice[t])
            owned = owned * ice[t]
            for d in range(4):
                fine.side[d, k, t] = owned * around[t][d]
    for t in both:
        fine.cross[t] = misc[2, t] * misc[3, t] * ice[t]
    for finer, coarser in ((fine, middle), (middle, column)):
        size = finer.depth // coarser.depth
        for k in range(coarser.depth):
            group = range(k * size, (k + 1) * size)
            diag = sum(finer.diag[j] for j in group)
            inner_faces = sum(finer.vert[j] for j in list(group)[:-1])
            coarser.diag[k] = diag - 2.0 * inner_faces
            if k + 1 < coarser.depth:
                coarser.vert[k] = finer.vert[group[-1]]
            for d in range(4):
                coarser.side[d, k] = sum(finer.side[d, j] for j in group)
        coarser.cross[...] = finer.cross[...]

    side2 = [column.side[d, 0, 0, own] for d in range(4)]
    diag2, cross2 = column.diag[0, 0, own], column.cross[0, own]
    inner = (diag2 - jnp.where(row < cx - 1, side2[0], 0.0) - jnp.where(row > 0, side2[1], 0.0)
             - jnp.where(lane < cy - 1, side2[2], 0.0) - jnp.where(lane > 0, side2[3], 0.0))
    entries = (inner, cross2, jnp.where(row == cx - 1, side2[0], 0.0), jnp.where(row == 0, side2[1], 0.0),
               jnp.where(last_lane, side2[2], 0.0), jnp.where(first_lane, side2[3], 0.0))
    eight = lax.broadcasted_iota(jnp.int32, (8, cy), 0)
    tile = jnp.zeros((8, cy), F32)
    for i, entry in enumerate(entries):
        tile = jnp.where(eight == i, total(entry), tile)
    gathers[2][0][...] = tile
    tables_start, tables_wait = gather(2)
    tables_start()
    for level in (fine, middle, column):
        level.factor()

    down = lax.broadcasted_iota(jnp.int32, (cy, cy), 0)
    across = lax.broadcasted_iota(jnp.int32, (cy, cy), 1)
    for r in range(cx):
        hit[r] = jnp.where(ids[r:r + 1, :] == down, 1.0, 0.0).astype(BF16)
    near = jnp.zeros((cy, cy), F32)
    for r in range(cx):
        here = hit[r].astype(F32)
        term = diag2[r:r + 1, :] * here
        if r + 1 < cx:
            term = term - side2[0][r:r + 1, :] * hit[r + 1].astype(F32)
        if r > 0:
            term = term - side2[1][r:r + 1, :] * hit[r - 1].astype(F32)
        term = term - jnp.where(across < cy - 1, side2[2][r:r + 1, :], 0.0) * pltpu.roll(here, cy - 1, 1)
        term = term - jnp.where(across > 0, side2[3][r:r + 1, :], 0.0) * pltpu.roll(here, 1, 1)
        high, low = split(term)
        near = near + dot(high, hit[r], 1, 1) + dot(low, hit[r], 1, 1)
    point_diag[...] = jnp.sum(jnp.where(down == across, near, 0.0), axis=0, keepdims=True)
    tables = [near]
    for d, r, e in ((0, cx - 1, HALO + cx), (1, 0, HALO - 1)):
        other = ids_all[0][e:e + 1, :]
        term = jnp.where(other == down, side2[d][r:r + 1, :], 0.0)
        high, low = split(term)
        tables.append(-(dot(high, hit[r], 1, 1) + dot(low, hit[r], 1, 1)))
    for d, q, e in ((2, cy - 1, 0), (3, 0, cy - 1)):
        other = ids_all[1][HALO:HALO + cx, e:e + 1]
        term = jnp.where(other == lane, side2[d][:, q:q + 1], 0.0)
        here = jnp.where(ids[:, q:q + 1] == lane, 1.0, 0.0)
        high, low = split(term)
        here = here.astype(BF16)
        tables.append(-(dot(high, here, 0, 0) + dot(low, here, 0, 0)))
    for i, table in enumerate(tables):
        high, low = split(table)
        big_hi[i] = high
        big_lo[i] = low

    tall4 = lax.broadcasted_iota(jnp.int32, (4 * cx, cy), 0) % cx

    def restrict_points(first, second):
        h0, l0 = split(first)
        h1, l1 = split(second)
        left = jnp.concatenate([h0, h1, l0, l1], axis=0)
        out = jnp.zeros((4 * cx, cy), F32)
        for r in range(cx):
            out = jnp.where(tall4 == r, dot(left, hit[r], 1, 1), out)
        parts = [jnp.sum(out[i * cx:(i + 1) * cx] + out[(i + 2) * cx:(i + 3) * cx], axis=0, keepdims=True)
                 for i in range(2)]
        return jnp.concatenate(parts, axis=0)

    point_cross[...] = restrict_points(cross2, cross2)
    block_row = lax.broadcasted_iota(jnp.int32, (count, cy), 0)

    def coarse_correction(j, left):
        sums = jnp.sum(left, axis=1, keepdims=True)
        gathers[0][0][...] = jnp.where(wide % 2 == 0, sums[0:1], sums[1:2])
        slot = lax.rem(j, 2)
        start, wait = gather(0, slot)
        start()
        pl.when(j == 0)(tables_wait)
        wait()
        right = gathers[0][1][slot, :, 0, :]
        diag, crossed, east, west, north, south = (gathers[2][1][0, :, i, :] for i in range(6))
        answer = COARSE_WEIGHT * right / diag
        for _ in range(CSWEEPS - 1):
            applied = diag * answer + crossed * pltpu.roll(answer, 1, 1) - (
                east * pltpu.roll(answer, count - ny, 0) + west * pltpu.roll(answer, ny, 0)
                + north * pltpu.roll(answer, count - 1, 0) + south * pltpu.roll(answer, 1, 0))
            answer = answer + COARSE_WEIGHT * (right - applied) / diag
        found = []
        for at in (me, me + ny, me - ny, me + 1, me - 1):
            line = jnp.sum(jnp.where(block_row == at, answer, 0.0), axis=0, keepdims=True)
            found.append(jnp.concatenate([line[:, 0:1], line[:, 1:2]], axis=0))
        return found

    def point_apply(xs):
        out = point_cross[...] * jnp.concatenate([xs[0][1:2], xs[0][0:1]], axis=0)
        for i, x in enumerate(xs):
            high, low = split(x)
            out = out + dot(high, big_hi[i], 1, 0) + dot(low, big_hi[i], 1, 0) + dot(high, big_lo[i], 1, 0)
        return out

    def point_cycle(j, right):
        def begin(p, x):
            x_out[p] = x
            q = lax.rem(p + j, 2)
            swap = near_swap(p, q)
            swap.start()

            def end():
                swap.wait()
                return [x] + [x_in[q, BACK[d]] for d in range(4)]
            return end

        scale = POINT_WEIGHT / point_diag[...]
        x = right * scale
        end = begin(0, x)
        packer = Packer(side_pack)
        for v in range(2):
            packer.add(column.field[1, 0, 0, v, pl.ds(TOP + HALO, cx), :])
            packer.add(column.right[0, 0, v, own])
        for k in range(half):
            for v in range(2):
                packer.add(middle.field[1, k, 0, v, pl.ds(TOP + HALO, cx), :])
        packer.finish()
        swap_side.start()
        x = x + (right - point_apply(end())) * scale
        xs = begin(1, x)()
        found = coarse_correction(j, right - point_apply(xs))
        xs = [x + y for x, y in zip(xs, found)]
        x = xs[0] + (right - point_apply(xs)) * scale
        return x + (right - point_apply(begin(0, x)())) * scale

    def spread_points(x):
        far_out[...] = x
        swap_far.start()
        swap_side.wait()
        swap_far.wait()
        parts = [[], []]
        zones = ((pl.ds(0, HALO), 1, 6, 7), (own, None, 2, 3), (pl.ds(HALO + cx, HALO), 0, 4, 5))
        short = {n: lax.broadcasted_iota(jnp.int32, (n, cy), 1) < cy // 2 for n in (HALO, cx)}

        def take(src, v, index):
            values = x if src is None else far_in[BACK[src]]
            return jnp.take_along_axis(jnp.broadcast_to(values[v:v + 1], index.shape), index, axis=1,
                                       mode="promise_in_bounds")

        for rows, straight, right, left in zones:
            index = [misc[1, t, rows].astype(jnp.int32) for t in both]
            parts[0].append(jnp.stack([take(straight, v, index[0]) for v in range(2)]))
            lanes = short[index[1].shape[0]]
            parts[1].append(jnp.stack([jnp.where(lanes, take(right, v, index[1]), take(left, v, index[1]))
                                       for v in range(2)]))
        return [jnp.concatenate(p, axis=1) for p in parts]

    def iteration(j, carry):
        def right0(k, t, here):
            return basis[j, :, k, t, here]

        def right1(k, t, here):
            return middle.right[k, t, :, here]

        def right2(k, t, here):
            return column.right[k, t, :, here]

        def collect(coarser, size):
            held = {}

            def emit(k, t, c0, cn, value):
                held[t] = held[t] + value if k % size else value
                if k % size == size - 1:
                    coarser.right[k // size, t, :, pl.ds(c0, cn)] = held[t]
            return emit

        fine.first(right0)
        fine.sweep(0, right0)
        fine.leftover(1, right0, collect(middle, 2))
        middle.first(right1)
        middle.sweep(0, right1)
        middle.leftover(1, right1, collect(column, half))
        column.first(right2)
        column.sweep(0, right2)
        kept = []
        column.leftover(1, right2, lambda k, t, c0, cn, value: kept.append(value), (0,), ((HALO, cx),))
        found = spread_points(point_cycle(j, restrict_points(kept[0][0], kept[0][1])))

        whole = pl.ds(TOP, tall)
        inside = pl.ds(TOP + HALO, cx)
        landed = []
        unpack(side_land, [landed.append] * (4 + 2 * half))
        column.field[0, 0, 0, :, whole] = found[0] + jnp.concatenate(
            [col_rows[0, 0], column.field[1, 0, 0, :, inside], col_rows[1, 0]], axis=1)
        column.field[0, 0, 1, :, whole] = found[1] + jnp.stack([landed[0], landed[2]])
        for e in range(2):
            column.right[0, 0, :, ends(e)] = col_rows[e, 1]
        column.right[0, 1] = jnp.stack([landed[1], landed[3]])
        column.after(right2)
        for k in range(half):
            middle.field[0, k, 0, :, whole] = column.field[0, 0, 0, :, whole] + jnp.concatenate(
                [mid_rows[0, k], middle.field[1, k, 0, :, inside], mid_rows[1, k]], axis=1)
            middle.field[0, k, 1, :, whole] = column.field[0, 0, 1, :, whole] + jnp.stack(
                [landed[4 + 2 * k], landed[5 + 2 * k]])
        middle.after(right1)
        for k in range(layers):
            for t in both:
                fine.field[0, k, t, :, whole] = (fine.field[1, k, t, :, whole]
                                                 + middle.field[0, k // 2, t, :, whole])
        fine.after(right0)

        packer = Packer(right_pack)

        def emit(k, t, c0, cn, value):
            basis[j + 1, :, k, 0, own] = value
            stored[j, :, k] = fine.field[0, k, 0, :, inside]
            for v in range(2):
                packer.add(value[v])

        fine.leftover(0, right0, emit, (0,), ((HALO, cx),))
        packer.finish()

        @pl.when(j < ITERS - 1)
        def _():
            swap = swap_right(j + 1)
            swap.start()
            swap.wait()
            unpack(right_land, [put_to(basis, j + 1, v, k, 1) for k in range(layers) for v in range(2)])
        return carry

    lax.fori_loop(0, ITERS, iteration, 0)

    names = [(i, j) for i in range(ITERS + 1) for j in range(i, ITERS + 1)]
    sums = {name: jnp.zeros((cx, cy), F32) for name in names}
    for k in range(layers):
        chain = [basis[i, :, k, 0, own] for i in range(ITERS + 1)]
        terms = [chain[j] - chain[j + 1] for j in range(ITERS)] + [chain[0]]
        for i, j in names:
            prod = terms[i] * terms[j]
            sums[i, j] = sums[i, j] + prod[0] + prod[1]
    line = reduce_all([total(sums[name]) for name in names])
    gram = {name: pick(line, at) for at, name in enumerate(names)}
    rows = [[gram[min(i, j), max(i, j)] for j in range(ITERS + 1)] for i in range(ITERS)]
    for a in range(ITERS):
        for i in range(a + 1, ITERS):
            share = rows[i][a] / rows[a][a]
            for c in range(a, ITERS + 1):
                rows[i][c] = rows[i][c] - share * rows[a][c]
    weights = [None] * ITERS
    for a in reversed(range(ITERS)):
        part = rows[a][ITERS]
        for c in range(a + 1, ITERS):
            part = part - rows[a][c] * weights[c]
        weights[a] = part / rows[a][a]
    for k in range(layers):
        out = weights[0] * stored[0, :, k]
        rest = forcing[:, k] - weights[0] * (basis[0, :, k, 0, own] - basis[1, :, k, 0, own])
        for j in range(1, ITERS):
            out = out + weights[j] * stored[j, :, k]
            rest = rest - weights[j] * (basis[j, :, k, 0, own] - basis[j + 1, :, k, 0, own])
        solution[:, k] = out
        residual[:, k] = rest


def solution(mesh):
    nx, ny = mesh.shape["gx"], mesh.shape["gy"]
    count = nx * ny

    def body(forcing, viscosity, spread, coupling, friction, mask, aggs):
        layers, cx, cy = forcing.shape[1:]
        dma = pltpu.SemaphoreType.DMA
        tall = cx + 2 * HALO
        half = layers // 2

        def vm(*shape, dtype=F32):
            return pltpu.VMEM(shape, dtype)

        def level(n):
            return (
                vm(2, n, 2, 2, tall + 2 * TOP, cy),
                vm(n, 2, tall, cy), vm(n, 2, tall, cy), vm(4, n, 2, tall, cy), vm(2, tall, cy),
                vm(n, 2, tall, cy), vm(n, 2, tall, cy), vm(n, 2, 2, tall, cy), vm(n, 2, 2, tall, cy),
            )

        def swap(planes, pieces):
            tiles = -(-planes * SLOT // cy)
            return (vm(tiles, cx, cy), vm(2, tiles, tall, cy), dma((8, pieces)), dma((8, pieces)))

        scratch = (
            (level(layers), level(half), level(1)),
            (vm(ITERS + 1, 2, layers, 2, tall, cy), vm(ITERS, 2, layers, cx, cy),
             vm(layers, 2, tall, cy), vm(layers, 2, tall, cy), vm(4, 2, tall, cy)),
            (vm(cx, cy, cy, dtype=BF16), vm(5, cy, cy, dtype=BF16), vm(5, cy, cy, dtype=BF16),
             vm(1, cy), vm(2, cy)),
            (vm(2, 2, cy), vm(2, 4, 2, cy), dma((2, 4, 1)), dma((2, 4, 1))),
            tuple((vm(n, cy), vm(2, count, n, cy), dma(()), dma((2,))) for n in (1, 1, 8)),
            swap(4 + 4 * layers, 4),
            swap(2 * layers, 1),
            swap(4 + 2 * half, 3),
            (vm(2, cy), vm(8, 2, cy), dma((8, 1)), dma((8, 1))),
            (vm(2, half, 2, HALO, cy), vm(2, 2, 2, HALO, cy)),
        )
        flat, tree = jax.tree.flatten(scratch)

        def run(*refs):
            kernel(nx, ny, layers, cx, cy, *refs[:9], *jax.tree.unflatten(tree, refs[9:]))

        shape = jax.ShapeDtypeStruct(forcing.shape, F32)
        whole = pl.BlockSpec(memory_space=pltpu.VMEM)
        return tuple(pl.pallas_call(
            run,
            out_shape=(shape, shape),
            in_specs=[whole] * 7,
            out_specs=(whole, whole),
            scratch_shapes=flat,
            compiler_params=pltpu.CompilerParams(has_side_effects=True, vmem_limit_bytes=60 * 1024 * 1024),
        )(forcing, viscosity, spread, coupling, friction, mask, aggs))

    return jax.shard_map(
        body,
        mesh=mesh,
        in_specs=(
            P(None, None, "gx", "gy"),
            P(None, "gx", "gy"),
            P(None, "gx", "gy"),
            P("gx", "gy"),
            P("gx", "gy"),
            P("gx", "gy"),
            P("gx", "gy"),
        ),
        out_specs=(P(None, None, "gx", "gy"), P(None, None, "gx", "gy")),
        check_vma=False,
    )
```

profile of v0, /device:TPU:0, one launch (start us, length us, event | category | flops | bytes accessed | tf_op | source)
XLA Modules:
  0.0 125.9 jit_solution(2548827965431413917)
XLA Ops:
  0.6 122.8 %shard_map.86 = (f32[2,20,16,128]{3,2,1,0:T(8,128)}, f32[2,20,16,128]{3,2,1,0:T(8,128)}) custom-call(f32[2,20,16,128]{3,2,1,0:T(8,128)} %refs_0_.1, f32[20,16,128]{2,1,0:T(8,128)} %refs_1_.1, f32[20,16,128]{2,1,0:T(8,128)} %refs_2_.1, f32[16,128]{1,0:T(8,128)} %refs_3_.1, f32[16,128]{1,0:T(8,128)} %refs_4_.1, s32[16,128]{1,0:T(8,128)} %refs_5_.1, ...), custom_call_target="tpu_custom_call" | custom-call | tf_op jit(solution)/shard_map/pallas_call | solution.py:698
  123.4 0.0 copy-start
  123.4 1.8 %copy.11 = f32[2,20,16,128]{3,2,1,0:T(8,128)} copy(f32[2,20,16,128]{3,2,1,0:T(8,128)} %get-tuple-element.4) | data formatting | bytes 655360
  125.2 0.0 copy-done
  125.2 0.7 copy.12
Async XLA Ops:
  123.4 1.8 %copy-start = (f32[2,20,16,128]{3,2,1,0:T(8,128)S(1)}, f32[2,20,16,128]{3,2,1,0:T(8,128)}, u32[]{:S(2)}) copy-start(f32[2,20,16,128]{3,2,1,0:T(8,128)} %get-tuple-element.5) | copy-start | bytes 983044
where the time goes:
time: 126 us
  Pallas kernels  123 us (98%)
  local copies, waits for them, and re-layouts  2.49 us (2%)
    pallas_call x1, Pallas kernels, body(): pl.pallas_call(run, out_shape=(shape, shape), in_specs=[whole] * 7, out_s...  123 us

commit v1 on v0

--- a/solution.py
+++ b/solution.py
@@ -44,9 +44,9 @@
     gx = lax.axis_index("gx")
     gy = lax.axis_index("gy")
     me = gx * ny + gy
-    (levels, (basis, stored, visc, spr, misc), (hit, big_hi, big_lo, point_diag, point_cross),
+    (levels, (basis, stored, visc, spr, misc), (hit, big_hi, big_lo, point_diag, point_cross, own_sum),
      (x_out, x_in, x_send, x_recv), gathers, first_swap, right_swap, side_swap, point_swap,
-     (mid_rows, col_rows)) = scratch
+     (mid_rows, col_rows), (near_out, near_in, near_send, near_recv)) = scratch
     tall = cx + 2 * HALO
     own = pl.ds(HALO, cx)
     slots = cy // SLOT
@@ -248,7 +248,6 @@
 
     (first_pack, first_land, first_send, first_recv) = first_swap
     swap0 = Swap(edges([
-        (lambda lo: forcing.at[:, :, pl.ds(lo, HALO)], lambda e: basis.at[0, :, :, 0, ends(e)]),
         (lambda lo: viscosity.at[:, pl.ds(lo, HALO)], lambda e: visc.at[:, 0, ends(e)]),
         (lambda lo: spread.at[:, pl.ds(lo, HALO)], lambda e: spr.at[:, 0, ends(e)]),
         (lambda lo: misc.at[:, 0, pl.ds(HALO + lo, HALO)], lambda e: misc.at[:, 0, ends(e)]),
@@ -268,6 +267,8 @@
     ], side_pack, side_land), side_send, side_recv)
     (far_out, far_in, far_send, far_recv) = point_swap
     swap_far = Swap([[(far_out, far_in.at[d])] for d in range(8)], far_send, far_recv)
+
+    swap_near = Swap([[(near_out, near_in.at[d])] for d in range(4)], near_send, near_recv)
 
     def near_swap(p, q):
         return Swap([[(x_out.at[p], x_in.at[q, d])] for d in range(4)], x_send.at[p], x_recv.at[q])
@@ -283,22 +284,26 @@
     for k in range(layers):
         packer.add(viscosity[k])
         packer.add(spread[k])
+    packer.finish()
+    swap0.start(range(2, 8))
+    packer = Packer(right_pack)
     for k in range(layers):
+        basis[0, :, k, 0, own] = forcing[:, k]
         for v in range(2):
             packer.add(forcing[v, k])
     packer.finish()
-    swap0.start(range(2, 8))
-    for j in range(1, ITERS):
+    swap_right(0).start()
+    for j in range(ITERS):
         swap_right(j).clear()
     swap0.clear()
     swap_side.clear()
     swap_far.clear()
     for q in range(2):
         near_swap(0, q).clear()
+    swap_near.clear()
     for k in range(layers):
         visc[k, 0, own] = viscosity[k]
         spr[k, 0, own] = spread[k]
-        basis[0, :, k, 0, own] = forcing[:, k]
 
     def gather(which, slot=0):
         out, into, send, recv = gathers[which]
@@ -346,8 +351,6 @@
     puts = [put_to(misc, i, 1) for i in range(4)]
     for k in range(layers):
         puts += [put_to(visc, k, 1), put_to(spr, k, 1)]
-    for k in range(layers):
-        puts += [put_to(basis, 0, v, k, 1) for v in range(2)]
     unpack(first_land, puts)
 
     ids_all = [misc[1, t].astype(jnp.int32) for t in both]
@@ -459,28 +462,70 @@
         return jnp.concatenate(parts, axis=0)
 
     point_cross[...] = restrict_points(cross2, cross2)
+    scale = POINT_WEIGHT / point_diag[...]
+    ones = jnp.ones((8, cy), BF16)
+    sixteen = lax.broadcasted_iota(jnp.int32, (16, cy), 0)
+    sent = jnp.where(sixteen == 5, scale * point_cross[0:1, :], 0.0)
+    for i, table in enumerate(tables):
+        sent = jnp.where(sixteen == i, scale * jnp.sum(table, axis=0, keepdims=True), sent)
+        across_sum = (dot(ones, big_hi[i], 1, 1) + dot(ones, big_lo[i], 1, 1))[0:1, :]
+        if i == 0:
+            own_sum[...] = across_sum
+        else:
+            sent = jnp.where(sixteen == 5 + i, across_sum, sent)
+    near_out[...] = sent
+    swap_near.start()
     block_row = lax.broadcasted_iota(jnp.int32, (count, cy), 0)
-
-    def coarse_correction(j, left):
-        sums = jnp.sum(left, axis=1, keepdims=True)
-        gathers[0][0][...] = jnp.where(wide % 2 == 0, sums[0:1], sums[1:2])
-        slot = lax.rem(j, 2)
-        start, wait = gather(0, slot)
+    coarse_lane = lax.broadcasted_iota(jnp.int32, (count, cy), 1)
+    shifts = (ny, count - ny, 1, count - 1)
+
+    def coarse_begin(j, right, x):
+        lines = [right - own_sum[...] * x - point_cross[...] * jnp.concatenate([x[1:2], x[0:1]], axis=0)]
+        for d in range(4):
+            lines.append(-near_in[BACK[d], 6 + BACK[d]:7 + BACK[d], :] * x)
+        line = jnp.zeros((1, cy), F32)
+        for i, part in enumerate(lines):
+            sums = jnp.sum(part, axis=1, keepdims=True)
+            for v in range(2):
+                line = jnp.where(wide == 2 * i + v, sums[v:v + 1], line)
+        gathers[0][0][...] = line
+        start, wait = gather(0, lax.rem(j, 2))
         start()
+        return wait
+
+    def coarse_end(j, wait):
         pl.when(j == 0)(tables_wait)
         wait()
-        right = gathers[0][1][slot, :, 0, :]
+        came = gathers[0][1][lax.rem(j, 2), :, 0, :]
+        right = came
+        for d in range(4):
+            right = right + pltpu.roll(pltpu.roll(came, shifts[d], 0), cy - 2 - 2 * d, 1)
         diag, crossed, east, west, north, south = (gathers[2][1][0, :, i, :] for i in range(6))
-        answer = COARSE_WEIGHT * right / diag
+        weight = COARSE_WEIGHT / diag
+        answer = right * weight
         for _ in range(CSWEEPS - 1):
-            applied = diag * answer + crossed * pltpu.roll(answer, 1, 1) - (
+            other = jnp.where(coarse_lane % 2 == 0, pltpu.roll(answer, cy - 1, 1), pltpu.roll(answer, 1, 1))
+            applied = diag * answer + crossed * other - (
                 east * pltpu.roll(answer, count - ny, 0) + west * pltpu.roll(answer, ny, 0)
                 + north * pltpu.roll(answer, count - 1, 0) + south * pltpu.roll(answer, 1, 0))
-            answer = answer + COARSE_WEIGHT * (right - applied) / diag
+            answer = answer + (right - applied) * weight
+        hops = ((0, 0),) + STEPS[:4]
+        known = {}
+
+        def value(dx, dy):
+            if (dx, dy) not in known:
+                line = jnp.sum(jnp.where(block_row == me + dx * ny + dy, answer, 0.0), axis=0, keepdims=True)
+                known[dx, dy] = jnp.concatenate([line[:, 0:1], line[:, 1:2]], axis=0)
+            return known[dx, dy]
+
         found = []
-        for at in (me, me + ny, me - ny, me + 1, me - 1):
-            line = jnp.sum(jnp.where(block_row == at, answer, 0.0), axis=0, keepdims=True)
-            found.append(jnp.concatenate([line[:, 0:1], line[:, 1:2]], axis=0))
+        for i, (dx, dy) in enumerate(hops):
+            here = value(dx, dy)
+            rows = near_out if i == 0 else near_in.at[BACK[i - 1]]
+            out = here - rows[5:6, :] * jnp.concatenate([here[1:2], here[0:1]], axis=0)
+            for n, (ex, ey) in enumerate(hops):
+                out = out - rows[n:n + 1, :] * value(dx + ex, dy + ey)
+            found.append(out)
         return found
 
     def point_apply(xs):
@@ -515,11 +560,13 @@
         packer.finish()
         swap_side.start()
         x = x + (right - point_apply(end())) * scale
-        xs = begin(1, x)()
-        found = coarse_correction(j, right - point_apply(xs))
-        xs = [x + y for x, y in zip(xs, found)]
-        x = xs[0] + (right - point_apply(xs)) * scale
-        return x + (right - point_apply(begin(0, x)())) * scale
+        end = begin(1, x)
+        pl.when(j == 0)(swap_near.wait)
+        coarse_wait = coarse_begin(j, right, x)
+        x = x + (right - point_apply(end())) * scale
+        xs = begin(0, x)()
+        xs = [x + y for x, y in zip(xs, coarse_end(j, coarse_wait))]
+        return xs[0] + (right - point_apply(xs)) * scale
 
     def spread_points(x):
         far_out[...] = x
@@ -562,6 +609,8 @@
                     coarser.right[k // size, t, :, pl.ds(c0, cn)] = held[t]
             return emit
 
+        swap_right(j).wait()
+        unpack(right_land, [put_to(basis, j, v, k, 1) for k in range(layers) for v in range(2)])
         fine.first(right0)
         fine.sweep(0, right0)
         fine.leftover(1, right0, collect(middle, 2))
@@ -610,10 +659,7 @@
 
         @pl.when(j < ITERS - 1)
         def _():
-            swap = swap_right(j + 1)
-            swap.start()
-            swap.wait()
-            unpack(right_land, [put_to(basis, j + 1, v, k, 1) for k in range(layers) for v in range(2)])
+            swap_right(j + 1).start()
         return carry
 
     lax.fori_loop(0, ITERS, iteration, 0)
@@ -679,14 +725,15 @@
             (vm(ITERS + 1, 2, layers, 2, tall, cy), vm(ITERS, 2, layers, cx, cy),
              vm(layers, 2, tall, cy), vm(layers, 2, tall, cy), vm(4, 2, tall, cy)),
             (vm(cx, cy, cy, dtype=BF16), vm(5, cy, cy, dtype=BF16), vm(5, cy, cy, dtype=BF16),
-             vm(1, cy), vm(2, cy)),
+             vm(1, cy), vm(2, cy), vm(1, cy)),
             (vm(2, 2, cy), vm(2, 4, 2, cy), dma((2, 4, 1)), dma((2, 4, 1))),
             tuple((vm(n, cy), vm(2, count, n, cy), dma(()), dma((2,))) for n in (1, 1, 8)),
-            swap(4 + 4 * layers, 4),
+            swap(4 + 2 * layers, 3),
             swap(2 * layers, 1),
             swap(4 + 2 * half, 3),
             (vm(2, cy), vm(8, 2, cy), dma((8, 1)), dma((8, 1))),
             (vm(2, half, 2, HALO, cy), vm(2, 2, 2, HALO, cy)),
+            (vm(16, cy), vm(4, 16, cy), dma((4, 1)), dma((4, 1))),
         )
         flat, tree = jax.tree.flatten(scratch)
 

time: 126 us -> 111 us (0.88)
  Pallas kernels: 123 us -> 108 us
    pallas_call x1, Pallas kernels: 123 us -> 108 us  [body(): pl.pallas_call(run, out_shape=(shape, shape), in_specs=[whole] * 7, out_s...]
where the time goes in v1:
time: 111 us
  Pallas kernels  108 us (97%)
  local copies, waits for them, and re-layouts  2.49 us (2%)
    pallas_call x1, Pallas kernels, body(): pl.pallas_call(run, out_shape=(shape, shape), in_specs=[whole] * 7, out_s...  108 us
    unnamed x4, local copies, waits for them, and re-layouts  2.49 us

profile of v1, /device:TPU:0, one launch (start us, length us, event | category | flops | bytes accessed | tf_op | source)
XLA Modules:
  0.0 111.3 jit_solution(8307436549346705517)
XLA Ops:
  0.6 108.1 %shard_map.86 = (f32[2,20,16,128]{3,2,1,0:T(8,128)}, f32[2,20,16,128]{3,2,1,0:T(8,128)}) custom-call(f32[2,20,16,128]{3,2,1,0:T(8,128)} %refs_0_.1, f32[20,16,128]{2,1,0:T(8,128)} %refs_1_.1, f32[20,16,128]{2,1,0:T(8,128)} %refs_2_.1, f32[16,128]{1,0:T(8,128)} %refs_3_.1, f32[16,128]{1,0:T(8,128)} %refs_4_.1, s32[16,128]{1,0:T(8,128)} %refs_5_.1, ...), custom_call_target="tpu_custom_call" | custom-call | tf_op jit(solution)/shard_map/pallas_call | solution.py:745
  108.8 0.0 copy-start
  108.8 1.8 %copy.11 = f32[2,20,16,128]{3,2,1,0:T(8,128)} copy(f32[2,20,16,128]{3,2,1,0:T(8,128)} %get-tuple-element.4) | data formatting | bytes 655360
  110.5 0.0 copy-done
  110.5 0.7 copy.12
Async XLA Ops:
  108.8 1.8 %copy-start = (f32[2,20,16,128]{3,2,1,0:T(8,128)S(1)}, f32[2,20,16,128]{3,2,1,0:T(8,128)}, u32[]{:S(2)}) copy-start(f32[2,20,16,128]{3,2,1,0:T(8,128)} %get-tuple-element.5) | copy-start | bytes 983044

commit v2 on v1

--- a/solution.py
+++ b/solution.py
@@ -16,6 +16,7 @@
 TOP = 8
 HALO = 8
 SLOT = 2 * HALO
+CHUNK = 16
 STEPS = ((1, 0), (-1, 0), (0, 1), (0, -1), (1, 1), (1, -1), (-1, 1), (-1, -1))
 BACK = (1, 0, 3, 2, 7, 6, 5, 4)
 
@@ -44,9 +45,10 @@
     gx = lax.axis_index("gx")
     gy = lax.axis_index("gy")
     me = gx * ny + gy
-    (levels, (basis, stored, visc, spr, misc), (hit, big_hi, big_lo, point_diag, point_cross, own_sum),
+    (levels, (basis, stored, visc, spr, misc, ice_ext), (hit, big, point_diag, point_cross, own_sum),
      (x_out, x_in, x_send, x_recv), gathers, first_swap, right_swap, side_swap, point_swap,
-     (mid_rows, col_rows), (near_out, near_in, near_send, near_recv)) = scratch
+     (mid_rows, col_rows), (near_out, near_in, big_near, near_send, near_recv),
+     coarse_tab) = scratch
     tall = cx + 2 * HALO
     own = pl.ds(HALO, cx)
     slots = cy // SLOT
@@ -145,79 +147,78 @@
                 comb = jnp.where(south, landed[0, s], landed[1, s])
             put(jnp.where(kept_lane, pltpu.roll(comb, (cy - SLOT * m - HALO) % cy, 1), 0.0))
 
-    chunks = ((0, tall // 2), (tall // 2, tall // 2))
+    chunks = [pl.ds(i * CHUNK, CHUNK) for i in range(tall // CHUNK)]
     both = (0, 1)
 
     class Level:
         def __init__(self, depth, refs):
             self.depth = depth
-            (self.field, self.diag, self.vert, self.side, self.cross, self.inverse, self.upper,
-             self.right, self.forward) = refs
-
-        def at(self, p, k, t, c0, cn, shift=0):
-            return self.field[p, k, t, :, pl.ds(TOP + c0 + shift, cn), :]
-
-        def sideways(self, p, k, c0, cn, tiles):
-            here = pl.ds(c0, cn)
-            wide = lax.broadcasted_iota(jnp.int32, (2, cn, cy), 2)
-            value = [self.at(p, k, t, c0, cn) for t in both]
+            (self.seen, self.field, self.diag, self.vert, self.side, self.cross, self.inverse, self.upper,
+             self.right, self.forward, self.moved) = refs
+
+        def put(self, p, k, t, here, value):
+            self.field[p, k, t, :, here] = value
+            self.seen[p, k, t, :, pl.ds(TOP + here.start, here.size)] = value * ice_ext[t, here][None]
+
+        def sideways(self, p, k, here, tiles):
+            def at(t, shift):
+                return self.seen[p, k, t, :, pl.ds(TOP + here.start + shift, here.size)]
+
+            lanes = lax.broadcasted_iota(jnp.int32, (2, here.size, cy), 2)
+            value = [at(t, 0) for t in both]
             up = [turn(v, cy - 1) for v in value]
             down = [turn(v, 1) for v in value]
             outs = []
             for t in tiles:
-                north = jnp.where(wide == cy - 1, up[1 - t], up[t])
-                south = jnp.where(wide == 0, down[1 - t], down[t])
-                out = (self.side[0, k, t, here][None] * self.at(p, k, t, c0, cn, 1)
-                       + self.side[1, k, t, here][None] * self.at(p, k, t, c0, cn, -1)
-                       + self.side[2, k, t, here][None] * north + self.side[3, k, t, here][None] * south)
+                north = jnp.where(lanes == cy - 1, up[1 - t], up[t])
+                south = jnp.where(lanes == 0, down[1 - t], down[t])
+                out = self.side[k, t, here][None] * ((at(t, 1) + at(t, -1)) + (north + south))
                 if k == 0:
                     crossed = self.cross[t, here]
                     out = out - jnp.stack([crossed * value[t][1], crossed * value[t][0]])
                 outs.append(out)
-            return value, outs
-
-        def leftover(self, p, right, emit, tiles=both, spans=chunks):
-            for c0, cn in spans:
-                here = pl.ds(c0, cn)
+            return outs
+
+        def leftover(self, p, right, emit, tiles=both, spans=None):
+            for here in spans or chunks:
                 for k in range(self.depth):
-                    value, outs = self.sideways(p, k, c0, cn, tiles)
+                    outs = self.sideways(p, k, here, tiles)
                     for i, t in enumerate(tiles):
-                        out = outs[i] - self.diag[k, t, here][None] * value[t]
-                        if k + 1 < self.depth:
-                            out = out + self.vert[k, t, here][None] * self.at(p, k + 1, t, c0, cn)
-                        if k > 0:
-                            out = out + self.vert[k - 1, t, here][None] * self.at(p, k - 1, t, c0, cn)
-                        emit(k, t, c0, cn, right(k, t, here) + out)
-
-        def solve(self, source, old, p):
-            for c0, cn in chunks:
-                here = pl.ds(c0, cn)
+                        emit(k, t, here, (1.0 - LINE_WEIGHT) ** 2 * right(k, t, here)
+                             + (outs[i] - LINE_WEIGHT * self.moved[k, t, :, here]))
+
+        def solve(self, source, old, p, spans=None):
+            for here in spans or chunks:
                 last = [None, None]
                 for k in range(self.depth):
-                    values = source(k, c0, cn)
+                    values = source(k, here)
                     for t in both:
                         value = values[t]
                         if k > 0:
                             value = value + self.vert[k - 1, t, here][None] * last[t]
                         last[t] = value * self.inverse[k, t, here][None]
-                        self.forward[k, t, :, here] = last[t]
+                        if k + 1 < self.depth:
+                            self.forward[k, t, :, here] = last[t]
                 for k in reversed(range(self.depth)):
                     for t in both:
                         if k + 1 < self.depth:
                             last[t] = self.forward[k, t, :, here] - self.upper[k, t, here][None] * last[t]
                         value = LINE_WEIGHT * last[t]
                         if old is not None:
-                            value = value + (1.0 - LINE_WEIGHT) * self.at(old, k, t, c0, cn)
-                        self.field[p, k, t, :, pl.ds(TOP + c0, cn), :] = value
+                            value = value + (1.0 - LINE_WEIGHT) * self.field[old, k, t, :, here]
+                        self.put(p, k, t, here, value)
 
         def first(self, right):
-            self.solve(lambda k, c0, cn: [right(k, t, pl.ds(c0, cn)) for t in both], None, 0)
-
-        def sweep(self, p, right):
-            def source(k, c0, cn):
-                outs = self.sideways(p, k, c0, cn, both)[1]
-                return [right(k, t, pl.ds(c0, cn)) + outs[t] for t in both]
-            self.solve(source, p, 1 - p)
+            self.solve(lambda k, here: [right(k, t, here) for t in both], None, 0)
+
+        def sweep(self, p, right, keep=False, spans=None):
+            def source(k, here):
+                outs = self.sideways(p, k, here, both)
+                if keep:
+                    for t in both:
+                        self.moved[k, t, :, here] = outs[t]
+                return [right(k, t, here) + outs[t] for t in both]
+            self.solve(source, p, 1 - p, spans)
 
         def factor(self):
             inverse = 1.0 / self.diag[0]
@@ -228,9 +229,13 @@
                 inverse = 1.0 / (self.diag[k] + self.vert[k - 1] * ratio)
                 self.inverse[k] = inverse
 
-        def after(self, right):
-            self.sweep(0, right)
-            self.sweep(1, right)
+        def before(self, right):
+            self.first(right)
+            self.sweep(0, right, True)
+
+        def after(self, right, spans=None):
+            self.sweep(0, right, spans=spans)
+            self.sweep(1, right, spans=spans)
 
     half = layers // 2
     fine, middle, column = (Level(n, refs) for n, refs in zip((layers, half, 1), levels))
@@ -238,8 +243,8 @@
         for p in range(2):
             for k in range(level.depth):
                 for t in both:
-                    level.field[p, k, t, :, pl.ds(0, TOP), :] = jnp.zeros((2, TOP, cy), F32)
-                    level.field[p, k, t, :, pl.ds(TOP + tall, TOP), :] = jnp.zeros((2, TOP, cy), F32)
+                    level.seen[p, k, t, :, pl.ds(0, TOP), :] = jnp.zeros((2, TOP, cy), F32)
+                    level.seen[p, k, t, :, pl.ds(TOP + tall, TOP), :] = jnp.zeros((2, TOP, cy), F32)
 
     def rows_of(ref, at):
         return lambda start: ref.at[at + (pl.ds(start, HALO),)]
@@ -255,14 +260,14 @@
     (right_pack, right_land, right_send, right_recv) = right_swap
 
     def swap_right(j):
-        return Swap(edges([(lambda lo: basis.at[j, :, :, 0, pl.ds(HALO + lo, HALO)],
-                            lambda e: basis.at[j, :, :, 0, ends(e)])],
+        return Swap(edges([(lambda lo: basis.at[j, :, :, 0, pl.ds(HALO + lo + (2 if lo else 0), HALO - 2)],
+                            lambda e: basis.at[j, :, :, 0, pl.ds(2 if e == 0 else HALO + cx, HALO - 2)])],
                           right_pack, right_land), right_send, right_recv)
 
     (side_pack, side_land, side_send, side_recv) = side_swap
     swap_side = Swap(edges([
-        (lambda lo: middle.field.at[1, :, 0, :, pl.ds(TOP + HALO + lo, HALO)], lambda e: mid_rows.at[e]),
-        (lambda lo: column.field.at[1, 0, 0, :, pl.ds(TOP + HALO + lo, HALO)], lambda e: col_rows.at[e, 0]),
+        (lambda lo: middle.field.at[1, :, 0, :, pl.ds(HALO + lo, HALO)], lambda e: mid_rows.at[e]),
+        (lambda lo: column.field.at[1, 0, 0, :, pl.ds(HALO + lo, HALO)], lambda e: col_rows.at[e, 0]),
         (lambda lo: column.right.at[0, 0, :, pl.ds(HALO + lo, HALO)], lambda e: col_rows.at[e, 1]),
     ], side_pack, side_land), side_send, side_recv)
     (far_out, far_in, far_send, far_recv) = point_swap
@@ -295,6 +300,9 @@
     swap_right(0).start()
     for j in range(ITERS):
         swap_right(j).clear()
+        for k in range(layers):
+            basis[j, :, k, 0, 0:HALO - 6] = jnp.zeros((2, HALO - 6, cy), F32)
+            basis[j, :, k, 0, tall - HALO + 6:tall] = jnp.zeros((2, HALO - 6, cy), F32)
     swap0.clear()
     swap_side.clear()
     swap_far.clear()
@@ -347,6 +355,46 @@
             ref[at] = value
         return put
 
+    ids = aggs[...]
+    ice_own = mask[...].astype(F32)
+    down = lax.broadcasted_iota(jnp.int32, (cy, cy), 0)
+    across = lax.broadcasted_iota(jnp.int32, (cy, cy), 1)
+    spots = [pl.ds(r * cy, cy) for r in range(cx)]
+    for r in range(cx):
+        hit[:, spots[r]] = jnp.where(ids[r:r + 1, :] == down, 1.0, 0.0).astype(BF16)
+    flow = sum(spread[k] for k in range(layers))
+    cross2 = friction[...] * coupling[...] * ice_own
+    diag2 = ice_own * (4.0 * flow + friction[...]) + layers * (1.0 - ice_own)
+    flow = flow * ice_own
+    ahead = jnp.where(lane < cy - 1, flow * pltpu.roll(ice_own, cy - 1, 1), 0.0)
+    behind = jnp.where(lane > 0, flow * pltpu.roll(ice_own, 1, 1), 0.0)
+    near = jnp.zeros((cy, cy), F32)
+    for r in range(cx):
+        here = hit[:, spots[r]].astype(F32)
+        term = diag2[r:r + 1, :] * here
+        if r + 1 < cx:
+            term = term - flow[r:r + 1, :] * ice_own[r + 1:r + 2, :] * hit[:, spots[r + 1]].astype(F32)
+        if r > 0:
+            term = term - flow[r:r + 1, :] * ice_own[r - 1:r, :] * hit[:, spots[r - 1]].astype(F32)
+        term = term - ahead[r:r + 1, :] * pltpu.roll(here, cy - 1, 1)
+        term = term - behind[r:r + 1, :] * pltpu.roll(here, 1, 1)
+        high, low = split(term)
+        near = near + dot(high, hit[:, spots[r]], 1, 1) + dot(low, hit[:, spots[r]], 1, 1)
+    point_diag[...] = jnp.sum(jnp.where(down == across, near, 0.0), axis=0, keepdims=True)
+    tall4 = lax.broadcasted_iota(jnp.int32, (4 * cx, cy), 0) % cx
+
+    def restrict_points(first, second):
+        h0, l0 = split(first)
+        h1, l1 = split(second)
+        left = jnp.concatenate([h0, h1, l0, l1], axis=0)
+        left = jnp.concatenate([jnp.where(tall4 == r, left, jnp.zeros_like(left)) for r in range(cx)], axis=1)
+        out = dot(left, hit[...], 1, 1)
+        parts = [jnp.sum(out[i * cx:(i + 1) * cx] + out[(i + 2) * cx:(i + 3) * cx], axis=0, keepdims=True)
+                 for i in range(2)]
+        return jnp.concatenate(parts, axis=0)
+
+    point_cross[...] = restrict_points(cross2, cross2)
+
     swap0.wait()
     puts = [put_to(misc, i, 1) for i in range(4)]
     for k in range(layers):
@@ -354,16 +402,16 @@
     unpack(first_land, puts)
 
     ids_all = [misc[1, t].astype(jnp.int32) for t in both]
-    ids = misc[1, 0, own].astype(jnp.int32)
     ice = [misc[0, t] for t in both]
     for t in both:
-        column.field[1, 0, t, 0, pl.ds(TOP, tall), :] = ice[t]
+        ice_ext[t] = ice[t]
+        column.seen[1, 0, t, 0, pl.ds(TOP, tall), :] = ice[t]
     around = []
     ups = [turn(x, cy - 1) for x in ice]
     downs = [turn(x, 1) for x in ice]
     for t in both:
-        around.append((column.field[1, 0, t, 0, pl.ds(TOP + 1, tall), :],
-                       column.field[1, 0, t, 0, pl.ds(TOP - 1, tall), :],
+        around.append((column.seen[1, 0, t, 0, pl.ds(TOP + 1, tall), :],
+                       column.seen[1, 0, t, 0, pl.ds(TOP - 1, tall), :],
                        jnp.where(long_lane == cy - 1, ups[1 - t], ups[t]),
                        jnp.where(long_lane == 0, downs[1 - t], downs[t])))
     for k in range(layers):
@@ -379,9 +427,7 @@
             if k == 0:
                 faces = faces + misc[2, t]
             fine.diag[k, t] = ice[t] * faces + (1.0 - ice[t])
-            owned = owned * ice[t]
-            for d in range(4):
-                fine.side[d, k, t] = owned * around[t][d]
+            fine.side[k, t] = owned * ice[t]
     for t in both:
         fine.cross[t] = misc[2, t] * misc[3, t] * ice[t]
     for finer, coarser in ((fine, middle), (middle, column)):
@@ -393,12 +439,10 @@
             coarser.diag[k] = diag - 2.0 * inner_faces
             if k + 1 < coarser.depth:
                 coarser.vert[k] = finer.vert[group[-1]]
-            for d in range(4):
-                coarser.side[d, k] = sum(finer.side[d, j] for j in group)
+            coarser.side[k] = sum(finer.side[j] for j in group)
         coarser.cross[...] = finer.cross[...]
 
-    side2 = [column.side[d, 0, 0, own] for d in range(4)]
-    diag2, cross2 = column.diag[0, 0, own], column.cross[0, own]
+    side2 = [column.side[0, 0, own] * around[0][d][HALO:HALO + cx] for d in range(4)]
     inner = (diag2 - jnp.where(row < cx - 1, side2[0], 0.0) - jnp.where(row > 0, side2[1], 0.0)
              - jnp.where(lane < cy - 1, side2[2], 0.0) - jnp.where(lane > 0, side2[3], 0.0))
     entries = (inner, cross2, jnp.where(row == cx - 1, side2[0], 0.0), jnp.where(row == 0, side2[1], 0.0),
@@ -413,29 +457,12 @@
     for level in (fine, middle, column):
         level.factor()
 
-    down = lax.broadcasted_iota(jnp.int32, (cy, cy), 0)
-    across = lax.broadcasted_iota(jnp.int32, (cy, cy), 1)
-    for r in range(cx):
-        hit[r] = jnp.where(ids[r:r + 1, :] == down, 1.0, 0.0).astype(BF16)
-    near = jnp.zeros((cy, cy), F32)
-    for r in range(cx):
-        here = hit[r].astype(F32)
-        term = diag2[r:r + 1, :] * here
-        if r + 1 < cx:
-            term = term - side2[0][r:r + 1, :] * hit[r + 1].astype(F32)
-        if r > 0:
-            term = term - side2[1][r:r + 1, :] * hit[r - 1].astype(F32)
-        term = term - jnp.where(across < cy - 1, side2[2][r:r + 1, :], 0.0) * pltpu.roll(here, cy - 1, 1)
-        term = term - jnp.where(across > 0, side2[3][r:r + 1, :], 0.0) * pltpu.roll(here, 1, 1)
-        high, low = split(term)
-        near = near + dot(high, hit[r], 1, 1) + dot(low, hit[r], 1, 1)
-    point_diag[...] = jnp.sum(jnp.where(down == across, near, 0.0), axis=0, keepdims=True)
     tables = [near]
     for d, r, e in ((0, cx - 1, HALO + cx), (1, 0, HALO - 1)):
         other = ids_all[0][e:e + 1, :]
         term = jnp.where(other == down, side2[d][r:r + 1, :], 0.0)
         high, low = split(term)
-        tables.append(-(dot(high, hit[r], 1, 1) + dot(low, hit[r], 1, 1)))
+        tables.append(-(dot(high, hit[:, spots[r]], 1, 1) + dot(low, hit[:, spots[r]], 1, 1)))
     for d, q, e in ((2, cy - 1, 0), (3, 0, cy - 1)):
         other = ids_all[1][HALO:HALO + cx, e:e + 1]
         term = jnp.where(other == lane, side2[d][:, q:q + 1], 0.0)
@@ -444,37 +471,56 @@
         here = here.astype(BF16)
         tables.append(-(dot(high, here, 0, 0) + dot(low, here, 0, 0)))
     for i, table in enumerate(tables):
-        high, low = split(table)
-        big_hi[i] = high
-        big_lo[i] = low
-
-    tall4 = lax.broadcasted_iota(jnp.int32, (4 * cx, cy), 0) % cx
-
-    def restrict_points(first, second):
-        h0, l0 = split(first)
-        h1, l1 = split(second)
-        left = jnp.concatenate([h0, h1, l0, l1], axis=0)
-        out = jnp.zeros((4 * cx, cy), F32)
-        for r in range(cx):
-            out = jnp.where(tall4 == r, dot(left, hit[r], 1, 1), out)
-        parts = [jnp.sum(out[i * cx:(i + 1) * cx] + out[(i + 2) * cx:(i + 3) * cx], axis=0, keepdims=True)
-                 for i in range(2)]
-        return jnp.concatenate(parts, axis=0)
-
-    point_cross[...] = restrict_points(cross2, cross2)
+        big[i * cy:(i + 1) * cy, 0:cy], big[i * cy:(i + 1) * cy, cy:2 * cy] = split(table)
+
     scale = POINT_WEIGHT / point_diag[...]
-    ones = jnp.ones((8, cy), BF16)
+    ones = jnp.ones((8, 2 * cy), BF16)
     sixteen = lax.broadcasted_iota(jnp.int32, (16, cy), 0)
     sent = jnp.where(sixteen == 5, scale * point_cross[0:1, :], 0.0)
     for i, table in enumerate(tables):
         sent = jnp.where(sixteen == i, scale * jnp.sum(table, axis=0, keepdims=True), sent)
-        across_sum = (dot(ones, big_hi[i], 1, 1) + dot(ones, big_lo[i], 1, 1))[0:1, :]
+        part = big[i * cy:(i + 1) * cy]
+        across_sum = dot(ones, part, 1, 1)[0:1, :]
         if i == 0:
             own_sum[...] = across_sum
         else:
             sent = jnp.where(sixteen == 5 + i, across_sum, sent)
-    near_out[...] = sent
+    sent = jnp.where(sixteen == 10, scale, sent)
+    near_out[0:16] = sent
+    edge_rows = jnp.zeros((8, cy), F32)
+    for i, (r, e) in enumerate(((cx - 1, HALO + cx), (0, HALO - 1))):
+        for n, line in enumerate((misc[1, 0, HALO + r:HALO + r + 1], misc[1, 0, e:e + 1], side2[i][r:r + 1])):
+            edge_rows = jnp.where(eight == 3 * i + n, line, edge_rows)
+    near_out[16:24] = edge_rows
+    edge_cols = jnp.zeros((cx, cy), F32)
+    for i, (q, e) in enumerate(((cy - 1, 0), (0, cy - 1))):
+        for n, line in enumerate((misc[1, 0, own, q:q + 1], misc[1, 1, own, e:e + 1], side2[2 + i][:, q:q + 1])):
+            edge_cols = jnp.where(lane == 3 * i + n, line, edge_cols)
+    near_out[24:24 + cx] = edge_cols
+    near_out[24 + cx:24 + cx + cy] = near
     swap_near.start()
+
+    def build_near():
+        swap_near.wait()
+        down_f, lane_f = down.astype(F32), lane.astype(F32)
+
+        def step(m, carry):
+            rows, cols = near_in[m, 16:24], near_in[m, 24:24 + cx]
+            found = [near_in[m, 24 + cx:24 + cx + cy]]
+            for i in range(2):
+                there = jnp.where(rows[3 * i:3 * i + 1] == down_f, 1.0, 0.0).astype(BF16)
+                high, low = split(jnp.where(rows[3 * i + 1:3 * i + 2] == down_f, rows[3 * i + 2:3 * i + 3], 0.0))
+                found.append(-(dot(high, there, 1, 1) + dot(low, there, 1, 1)))
+            for i in range(2):
+                there = jnp.where(cols[:, 3 * i:3 * i + 1] == lane_f, 1.0, 0.0).astype(BF16)
+                high, low = split(jnp.where(cols[:, 3 * i + 1:3 * i + 2] == lane_f, cols[:, 3 * i + 2:3 * i + 3], 0.0))
+                found.append(-(dot(high, there, 0, 0) + dot(low, there, 0, 0)))
+            for i, table in enumerate(found):
+                big_near[m, i * cy:(i + 1) * cy, 0:cy], big_near[m, i * cy:(i + 1) * cy, cy:2 * cy] = split(table)
+            return carry
+
+        lax.fori_loop(0, 4, step, 0)
+
     block_row = lax.broadcasted_iota(jnp.int32, (count, cy), 0)
     coarse_lane = lax.broadcasted_iota(jnp.int32, (count, cy), 1)
     shifts = (ny, count - ny, 1, count - 1)
@@ -488,20 +534,25 @@
             sums = jnp.sum(part, axis=1, keepdims=True)
             for v in range(2):
                 line = jnp.where(wide == 2 * i + v, sums[v:v + 1], line)
-        gathers[0][0][...] = line
+        gathers[0][0][0:2] = x
+        gathers[0][0][2:3] = line
         start, wait = gather(0, lax.rem(j, 2))
         start()
         return wait
 
     def coarse_end(j, wait):
-        pl.when(j == 0)(tables_wait)
+        @pl.when(j == 0)
+        def _():
+            tables_wait()
+            for i in range(6):
+                coarse_tab[i] = gathers[2][1][0, :, i, :]
+            coarse_tab[6] = COARSE_WEIGHT / coarse_tab[0]
         wait()
-        came = gathers[0][1][lax.rem(j, 2), :, 0, :]
+        came = gathers[0][1][lax.rem(j, 2), :, 2, :]
         right = came
         for d in range(4):
             right = right + pltpu.roll(pltpu.roll(came, shifts[d], 0), cy - 2 - 2 * d, 1)
-        diag, crossed, east, west, north, south = (gathers[2][1][0, :, i, :] for i in range(6))
-        weight = COARSE_WEIGHT / diag
+        diag, crossed, east, west, north, south, weight = (coarse_tab[i] for i in range(7))
         answer = right * weight
         for _ in range(CSWEEPS - 1):
             other = jnp.where(coarse_lane % 2 == 0, pltpu.roll(answer, cy - 1, 1), pltpu.roll(answer, 1, 1))
@@ -528,50 +579,75 @@
             found.append(out)
         return found
 
+    def swapped(x):
+        return jnp.concatenate([x[1:2], x[0:1]], axis=0)
+
+    def apply_tables(table, xs):
+        parts = [split(x) for x in xs]
+        left = jnp.concatenate([jnp.concatenate([p[i] for p in parts], axis=1) for i in range(2)], axis=0)
+        both_parts = dot(left, table[...], 1, 0)
+        both_parts = both_parts[0:2] + both_parts[2:4]
+        return both_parts[:, 0:cy] + both_parts[:, cy:2 * cy]
+
     def point_apply(xs):
-        out = point_cross[...] * jnp.concatenate([xs[0][1:2], xs[0][0:1]], axis=0)
-        for i, x in enumerate(xs):
-            high, low = split(x)
-            out = out + dot(high, big_hi[i], 1, 0) + dot(low, big_hi[i], 1, 0) + dot(high, big_lo[i], 1, 0)
-        return out
+        return point_cross[...] * swapped(xs[0]) + apply_tables(big, xs)
 
     def point_cycle(j, right):
-        def begin(p, x):
-            x_out[p] = x
-            q = lax.rem(p + j, 2)
-            swap = near_swap(p, q)
-            swap.start()
-
-            def end():
-                swap.wait()
-                return [x] + [x_in[q, BACK[d]] for d in range(4)]
-            return end
-
-        scale = POINT_WEIGHT / point_diag[...]
-        x = right * scale
-        end = begin(0, x)
+        x_out[0] = right * (POINT_WEIGHT / point_diag[...])
+        swap = near_swap(0, 0)
+        swap.start()
         packer = Packer(side_pack)
         for v in range(2):
-            packer.add(column.field[1, 0, 0, v, pl.ds(TOP + HALO, cx), :])
+            packer.add(column.field[1, 0, 0, v, own])
             packer.add(column.right[0, 0, v, own])
         for k in range(half):
             for v in range(2):
-                packer.add(middle.field[1, k, 0, v, pl.ds(TOP + HALO, cx), :])
+                packer.add(middle.field[1, k, 0, v, own])
         packer.finish()
         swap_side.start()
-        x = x + (right - point_apply(end())) * scale
-        end = begin(1, x)
-        pl.when(j == 0)(swap_near.wait)
+        pl.when(j == 0)(build_near)
+        scale = POINT_WEIGHT / point_diag[...]
+        swap.wait()
+        first = [right * scale] + [x_in[0, BACK[d]] for d in range(4)]
+        x = first[0] + (right - point_apply(first)) * scale
         coarse_wait = coarse_begin(j, right, x)
-        x = x + (right - point_apply(end())) * scale
-        xs = begin(0, x)()
-        xs = [x + y for x, y in zip(xs, coarse_end(j, coarse_wait))]
+        merge_side()
+        found = coarse_end(j, coarse_wait)
+        hops = ((0, 0),) + STEPS[:4]
+
+        def second(dx, dy):
+            return gathers[0][1][lax.rem(j, 2), lax.rem(me + dx * ny + dy + count, count), 0:2]
+
+        xs = []
+        for i, (dx, dy) in enumerate(hops):
+            local = [second(dx + ex, dy + ey) for ex, ey in hops]
+            if i == 0:
+                moved = point_apply(local) * scale
+            else:
+                rows = near_in.at[BACK[i - 1]]
+                moved = (rows[10:11] * apply_tables(big_near.at[BACK[i - 1]], local)
+                         + rows[5:6] * swapped(local[0]))
+            xs.append(local[0] + first[i] - moved + found[i])
         return xs[0] + (right - point_apply(xs)) * scale
+
+    def merge_side():
+        swap_side.wait()
+        column.field[0, 0, 0] = jnp.concatenate([col_rows[0, 0], column.field[1, 0, 0, :, own], col_rows[1, 0]], axis=1)
+        for e in range(2):
+            column.right[0, 0, :, ends(e)] = col_rows[e, 1]
+        for k in range(half):
+            middle.field[0, k, 0] = jnp.concatenate([mid_rows[0, k], middle.field[1, k, 0, :, own], mid_rows[1, k]],
+                                                    axis=1)
+        puts = []
+        for v in range(2):
+            puts += [put_to(column.field, 0, 0, 1, v), put_to(column.right, 0, 1, v)]
+        for k in range(half):
+            puts += [put_to(middle.field, 0, k, 1, v) for v in range(2)]
+        unpack(side_land, puts)
 
     def spread_points(x):
         far_out[...] = x
         swap_far.start()
-        swap_side.wait()
         swap_far.wait()
         parts = [[], []]
         zones = ((pl.ds(0, HALO), 1, 6, 7), (own, None, 2, 3), (pl.ds(HALO + cx, HALO), 0, 4, 5))
@@ -603,58 +679,50 @@
         def collect(coarser, size):
             held = {}
 
-            def emit(k, t, c0, cn, value):
+            def emit(k, t, here, value):
                 held[t] = held[t] + value if k % size else value
                 if k % size == size - 1:
-                    coarser.right[k // size, t, :, pl.ds(c0, cn)] = held[t]
+                    coarser.right[k // size, t, :, here] = held[t]
             return emit
 
         swap_right(j).wait()
         unpack(right_land, [put_to(basis, j, v, k, 1) for k in range(layers) for v in range(2)])
-        fine.first(right0)
-        fine.sweep(0, right0)
+        fine.before(right0)
         fine.leftover(1, right0, collect(middle, 2))
-        middle.first(right1)
-        middle.sweep(0, right1)
+        middle.before(right1)
         middle.leftover(1, right1, collect(column, half))
-        column.first(right2)
-        column.sweep(0, right2)
+        column.before(right2)
         kept = []
-        column.leftover(1, right2, lambda k, t, c0, cn, value: kept.append(value), (0,), ((HALO, cx),))
+        column.leftover(1, right2, lambda k, t, here, value: kept.append(value), (0,), (own,))
         found = spread_points(point_cycle(j, restrict_points(kept[0][0], kept[0][1])))
 
-        whole = pl.ds(TOP, tall)
-        inside = pl.ds(TOP + HALO, cx)
-        landed = []
-        unpack(side_land, [landed.append] * (4 + 2 * half))
-        column.field[0, 0, 0, :, whole] = found[0] + jnp.concatenate(
-            [col_rows[0, 0], column.field[1, 0, 0, :, inside], col_rows[1, 0]], axis=1)
-        column.field[0, 0, 1, :, whole] = found[1] + jnp.stack([landed[0], landed[2]])
-        for e in range(2):
-            column.right[0, 0, :, ends(e)] = col_rows[e, 1]
-        column.right[0, 1] = jnp.stack([landed[1], landed[3]])
+        whole = pl.ds(0, tall)
+        for t in both:
+            column.put(0, 0, t, whole, found[t] + column.field[0, 0, t])
         column.after(right2)
         for k in range(half):
-            middle.field[0, k, 0, :, whole] = column.field[0, 0, 0, :, whole] + jnp.concatenate(
-                [mid_rows[0, k], middle.field[1, k, 0, :, inside], mid_rows[1, k]], axis=1)
-            middle.field[0, k, 1, :, whole] = column.field[0, 0, 1, :, whole] + jnp.stack(
-                [landed[4 + 2 * k], landed[5 + 2 * k]])
+            for t in both:
+                middle.put(0, k, t, whole, column.field[0, 0, t] + middle.field[0, k, t])
         middle.after(right1)
         for k in range(layers):
             for t in both:
-                fine.field[0, k, t, :, whole] = (fine.field[1, k, t, :, whole]
-                                                 + middle.field[0, k // 2, t, :, whole])
-        fine.after(right0)
+                fine.put(0, k, t, whole, fine.field[1, k, t] + middle.field[0, k // 2, t])
+        fine.after(right0, [pl.ds(HALO // 2 + i * 8, 8) for i in range(cx // 8 + 1)])
 
         packer = Packer(right_pack)
 
-        def emit(k, t, c0, cn, value):
+        for k in range(layers):
+            here = fine.field[0, k, 0, :, own]
+            stored[j, :, k] = here
+            out = fine.sideways(0, k, own, (0,))[0] - fine.diag[k, 0, own][None] * here
+            if k + 1 < layers:
+                out = out + fine.vert[k, 0, own][None] * fine.field[0, k + 1, 0, :, own]
+            if k > 0:
+                out = out + fine.vert[k - 1, 0, own][None] * fine.field[0, k - 1, 0, :, own]
+            value = basis[j, :, k, 0, own] + out
             basis[j + 1, :, k, 0, own] = value
-            stored[j, :, k] = fine.field[0, k, 0, :, inside]
             for v in range(2):
                 packer.add(value[v])
-
-        fine.leftover(0, right0, emit, (0,), ((HALO, cx),))
         packer.finish()
 
         @pl.when(j < ITERS - 1)
@@ -692,8 +760,9 @@
         for j in range(1, ITERS):
             out = out + weights[j] * stored[j, :, k]
             rest = rest - weights[j] * (basis[j, :, k, 0, own] - basis[j + 1, :, k, 0, own])
-        solution[:, k] = out
-        residual[:, k] = rest
+        for v in range(2):
+            solution[pl.ds((v * layers + k) * cx, cx)] = out[v]
+            residual[pl.ds((v * layers + k) * cx, cx)] = rest[v]
 
 
 def solution(mesh):
@@ -711,9 +780,10 @@
 
         def level(n):
             return (
-                vm(2, n, 2, 2, tall + 2 * TOP, cy),
-                vm(n, 2, tall, cy), vm(n, 2, tall, cy), vm(4, n, 2, tall, cy), vm(2, tall, cy),
+                vm(2, n, 2, 2, tall + 2 * TOP, cy), vm(2, n, 2, 2, tall, cy),
+                vm(n, 2, tall, cy), vm(n, 2, tall, cy), vm(n, 2, tall, cy), vm(2, tall, cy),
                 vm(n, 2, tall, cy), vm(n, 2, tall, cy), vm(n, 2, 2, tall, cy), vm(n, 2, 2, tall, cy),
+                vm(n, 2, 2, tall, cy),
             )
 
         def swap(planes, pieces):
@@ -723,33 +793,35 @@
         scratch = (
             (level(layers), level(half), level(1)),
             (vm(ITERS + 1, 2, layers, 2, tall, cy), vm(ITERS, 2, layers, cx, cy),
-             vm(layers, 2, tall, cy), vm(layers, 2, tall, cy), vm(4, 2, tall, cy)),
-            (vm(cx, cy, cy, dtype=BF16), vm(5, cy, cy, dtype=BF16), vm(5, cy, cy, dtype=BF16),
+             vm(layers, 2, tall, cy), vm(layers, 2, tall, cy), vm(4, 2, tall, cy), vm(2, tall, cy)),
+            (vm(cy, cx * cy, dtype=BF16), vm(5 * cy, 2 * cy, dtype=BF16),
              vm(1, cy), vm(2, cy), vm(1, cy)),
             (vm(2, 2, cy), vm(2, 4, 2, cy), dma((2, 4, 1)), dma((2, 4, 1))),
-            tuple((vm(n, cy), vm(2, count, n, cy), dma(()), dma((2,))) for n in (1, 1, 8)),
+            tuple((vm(n, cy), vm(2, count, n, cy), dma(()), dma((2,))) for n in (3, 1, 8)),
             swap(4 + 2 * layers, 3),
             swap(2 * layers, 1),
             swap(4 + 2 * half, 3),
             (vm(2, cy), vm(8, 2, cy), dma((8, 1)), dma((8, 1))),
             (vm(2, half, 2, HALO, cy), vm(2, 2, 2, HALO, cy)),
-            (vm(16, cy), vm(4, 16, cy), dma((4, 1)), dma((4, 1))),
+            (vm(24 + cx + cy, cy), vm(4, 24 + cx + cy, cy), vm(4, 5 * cy, 2 * cy, dtype=BF16), dma((4, 1)), dma((4, 1))),
+            vm(7, count, cy),
         )
         flat, tree = jax.tree.flatten(scratch)
 
         def run(*refs):
             kernel(nx, ny, layers, cx, cy, *refs[:9], *jax.tree.unflatten(tree, refs[9:]))
 
-        shape = jax.ShapeDtypeStruct(forcing.shape, F32)
+        shape = jax.ShapeDtypeStruct((2 * layers * cx, cy), F32)
         whole = pl.BlockSpec(memory_space=pltpu.VMEM)
-        return tuple(pl.pallas_call(
+        outs = pl.pallas_call(
             run,
             out_shape=(shape, shape),
             in_specs=[whole] * 7,
             out_specs=(whole, whole),
             scratch_shapes=flat,
             compiler_params=pltpu.CompilerParams(has_side_effects=True, vmem_limit_bytes=60 * 1024 * 1024),
-        )(forcing, viscosity, spread, coupling, friction, mask, aggs))
+        )(forcing, viscosity, spread, coupling, friction, mask, aggs)
+        return tuple(out.reshape(forcing.shape) for out in outs)
 
     return jax.shard_map(
         body,

time: 111 us -> 101 us (0.910)
  Pallas kernels: 108 us -> 97.7 us
    pallas_call x1, Pallas kernels: 108 us -> 97.7 us  [body(): pl.pallas_call(run, out_shape=(shape, shape), in_specs=[whole] * 7, out_s...]
where the time goes in v2:
time: 101 us
  Pallas kernels  97.7 us (97%)
  local copies, waits for them, and re-layouts  2.49 us (2%)
    pallas_call x1, Pallas kernels, body(): pl.pallas_call(run, out_shape=(shape, shape), in_specs=[whole] * 7, out_s...  97.7 us
    unnamed x4, local copies, waits for them, and re-layouts  2.49 us

profile of v2, /device:TPU:0, one launch (start us, length us, event | category | flops | bytes accessed | tf_op | source)
XLA Modules:
  0.0 100.9 jit_solution(6709926821842963947)
XLA Ops:
  0.6 97.7 %shard_map.86 = (f32[640,128]{1,0:T(8,128)}, f32[640,128]{1,0:T(8,128)}) custom-call(f32[2,20,16,128]{3,2,1,0:T(8,128)} %refs_0_.1, f32[20,16,128]{2,1,0:T(8,128)} %refs_1_.1, f32[20,16,128]{2,1,0:T(8,128)} %refs_2_.1, f32[16,128]{1,0:T(8,128)} %refs_3_.1, f32[16,128]{1,0:T(8,128)} %refs_4_.1, s32[16,128]{1,0:T(8,128)} %refs_5_.1, s32[16,128]{1,0:T(8,128)} %refs_6_.1), custom_call_target="tpu_custom_call" | custom-call | tf_op jit(solution)/shard_map/pallas_call | solution.py:816
  98.4 0.0 copy-start
  98.4 1.8 %copy.11 = f32[2,20,16,128]{3,2,1,0:T(8,128)} copy(f32[2,20,16,128]{3,2,1,0:T(8,128)} %bitcast.3) | data formatting | bytes 655360
  100.1 0.0 copy-done
  100.2 0.7 copy.12
Async XLA Ops:
  98.4 1.8 %copy-start = (f32[640,128]{1,0:T(8,128)S(1)}, f32[640,128]{1,0:T(8,128)}, u32[]{:S(2)}) copy-start(f32[640,128]{1,0:T(8,128)} %get-tuple-element.5) | copy-start | bytes 983044

commit v3 on v2

--- a/solution.py
+++ b/solution.py
@@ -15,8 +15,8 @@
 BF16 = jnp.bfloat16
 TOP = 8
 HALO = 8
-SLOT = 2 * HALO
 CHUNK = 16
+INNER = 8
 STEPS = ((1, 0), (-1, 0), (0, 1), (0, -1), (1, 1), (1, -1), (-1, 1), (-1, -1))
 BACK = (1, 0, 3, 2, 7, 6, 5, 4)
 
@@ -40,7 +40,7 @@
 
 
 def kernel(nx, ny, layers, cx, cy, forcing, viscosity, spread, coupling, friction, mask, aggs,
-           solution, residual, *scratch):
+           result, *scratch):
     count = nx * ny
     gx = lax.axis_index("gx")
     gy = lax.axis_index("gy")
@@ -48,10 +48,10 @@
     (levels, (basis, stored, visc, spr, misc, ice_ext), (hit, big, point_diag, point_cross, own_sum),
      (x_out, x_in, x_send, x_recv), gathers, first_swap, right_swap, side_swap, point_swap,
      (mid_rows, col_rows), (near_out, near_in, big_near, near_send, near_recv),
-     coarse_tab) = scratch
+     coarse_tab, lift_side, lift_cross) = scratch
     tall = cx + 2 * HALO
     own = pl.ds(HALO, cx)
-    slots = cy // SLOT
+    slots = cy // HALO
     lane = lax.broadcasted_iota(jnp.int32, (cx, cy), 1)
     row = lax.broadcasted_iota(jnp.int32, (cx, cy), 0)
     first_lane, last_lane = lane == 0, lane == cy - 1
@@ -105,12 +105,12 @@
         return [
             [(src(cx - HALO), dst(0)) for src, dst in rows],
             [(src(0), dst(1)) for src, dst in rows],
-            [(packed, landed.at[0, :, own])],
-            [(packed, landed.at[1, :, own])],
-            [(packed.at[:, high], landed.at[0, :, top])],
-            [(packed.at[:, high], landed.at[1, :, top])],
-            [(packed.at[:, low], landed.at[0, :, bottom])],
-            [(packed.at[:, low], landed.at[1, :, bottom])],
+            [(packed.at[0], landed.at[0, :, own])],
+            [(packed.at[1], landed.at[1, :, own])],
+            [(packed.at[0, :, high], landed.at[0, :, top])],
+            [(packed.at[1, :, high], landed.at[1, :, top])],
+            [(packed.at[0, :, low], landed.at[0, :, bottom])],
+            [(packed.at[1, :, low], landed.at[1, :, bottom])],
         ]
 
     def ends(e):
@@ -120,32 +120,34 @@
         def __init__(self, out):
             self.out = out
             self.at = 0
-            self.tile = None
+            self.tiles = None
 
         def add(self, value):
             s, m = divmod(self.at, slots)
-            moved = pltpu.roll(value, (SLOT * m + HALO) % cy, 1)
-            self.tile = moved if m == 0 else jnp.where(lane // SLOT == m, moved, self.tile)
+            moved = pltpu.roll(value, (HALO * m + HALO) % cy, 1)
+            self.tiles = [moved] * 2 if m == 0 else [
+                jnp.where(lane // HALO == (m + i) % slots, moved, self.tiles[i]) for i in range(2)]
             self.at += 1
             if m == slots - 1:
                 self.flush(s)
 
         def flush(self, s):
-            self.out[s] = self.tile
-            self.tile = None
+            for i in range(2):
+                self.out[i, s] = self.tiles[i]
+            self.tiles = None
 
         def finish(self):
-            if self.tile is not None:
+            if self.tiles is not None:
                 self.flush((self.at - 1) // slots)
 
     def unpack(landed, puts):
-        south = long_lane % SLOT < HALO
+        south = long_lane // HALO % 2 == 0
         comb = None
         for i, put in enumerate(puts):
             s, m = divmod(i, slots)
             if m == 0:
-                comb = jnp.where(south, landed[0, s], landed[1, s])
-            put(jnp.where(kept_lane, pltpu.roll(comb, (cy - SLOT * m - HALO) % cy, 1), 0.0))
+                comb = [jnp.where(south, landed[e, s], landed[1 - e, s]) for e in range(2)]
+            put(jnp.where(kept_lane, pltpu.roll(comb[m % 2], (2 * cy - HALO * m - HALO) % cy, 1), 0.0))
 
     chunks = [pl.ds(i * CHUNK, CHUNK) for i in range(tall // CHUNK)]
     both = (0, 1)
@@ -160,7 +162,7 @@
             self.field[p, k, t, :, here] = value
             self.seen[p, k, t, :, pl.ds(TOP + here.start, here.size)] = value * ice_ext[t, here][None]
 
-        def sideways(self, p, k, here, tiles):
+        def sums(self, p, k, here, tiles):
             def at(t, shift):
                 return self.seen[p, k, t, :, pl.ds(TOP + here.start + shift, here.size)]
 
@@ -172,22 +174,29 @@
             for t in tiles:
                 north = jnp.where(lanes == cy - 1, up[1 - t], up[t])
                 south = jnp.where(lanes == 0, down[1 - t], down[t])
-                out = self.side[k, t, here][None] * ((at(t, 1) + at(t, -1)) + (north + south))
-                if k == 0:
+                outs.append((at(t, 1) + at(t, -1)) + (north + south))
+            return value, outs
+
+        def sideways(self, k, here, tiles, value, outs):
+            outs = [self.side[k, t, here][None] * out for t, out in zip(tiles, outs)]
+            if k == 0:
+                for i, t in enumerate(tiles):
                     crossed = self.cross[t, here]
-                    out = out - jnp.stack([crossed * value[t][1], crossed * value[t][0]])
-                outs.append(out)
+                    outs[i] = outs[i] - jnp.stack([crossed * value[t][1], crossed * value[t][0]])
             return outs
+
+        def beside(self, p, k, here, tiles):
+            return self.sideways(k, here, tiles, *self.sums(p, k, here, tiles))
 
         def leftover(self, p, right, emit, tiles=both, spans=None):
             for here in spans or chunks:
                 for k in range(self.depth):
-                    outs = self.sideways(p, k, here, tiles)
+                    outs = self.beside(p, k, here, tiles)
                     for i, t in enumerate(tiles):
                         emit(k, t, here, (1.0 - LINE_WEIGHT) ** 2 * right(k, t, here)
                              + (outs[i] - LINE_WEIGHT * self.moved[k, t, :, here]))
 
-        def solve(self, source, old, p, spans=None):
+        def solve(self, source, finish, spans):
             for here in spans or chunks:
                 last = [None, None]
                 for k in range(self.depth):
@@ -203,22 +212,27 @@
                     for t in both:
                         if k + 1 < self.depth:
                             last[t] = self.forward[k, t, :, here] - self.upper[k, t, here][None] * last[t]
-                        value = LINE_WEIGHT * last[t]
-                        if old is not None:
-                            value = value + (1.0 - LINE_WEIGHT) * self.field[old, k, t, :, here]
-                        self.put(p, k, t, here, value)
-
-        def first(self, right):
-            self.solve(lambda k, here: [right(k, t, here) for t in both], None, 0)
-
-        def sweep(self, p, right, keep=False, spans=None):
+                        finish(k, t, here, LINE_WEIGHT * last[t])
+
+        def first(self, right, spans=None):
+            self.solve(lambda k, here: [right(k, t, here) for t in both],
+                       lambda k, t, here, value: self.put(0, k, t, here, value), spans)
+
+        def sweep(self, p, right, keep=False, spans=None, plain=False):
             def source(k, here):
-                outs = self.sideways(p, k, here, both)
+                outs = self.beside(p, k, here, both)
                 if keep:
                     for t in both:
                         self.moved[k, t, :, here] = outs[t]
                 return [right(k, t, here) + outs[t] for t in both]
-            self.solve(source, p, 1 - p, spans)
+
+            def finish(k, t, here, value):
+                value = value + (1.0 - LINE_WEIGHT) * self.field[p, k, t, :, here]
+                if plain:
+                    self.field[1 - p, k, t, :, here] = value
+                else:
+                    self.put(1 - p, k, t, here, value)
+            self.solve(source, finish, spans)
 
         def factor(self):
             inverse = 1.0 / self.diag[0]
@@ -229,22 +243,19 @@
                 inverse = 1.0 / (self.diag[k] + self.vert[k - 1] * ratio)
                 self.inverse[k] = inverse
 
-        def before(self, right):
-            self.first(right)
-            self.sweep(0, right, True)
-
-        def after(self, right, spans=None):
-            self.sweep(0, right, spans=spans)
-            self.sweep(1, right, spans=spans)
-
+        def before(self, right, spans=None):
+            self.first(right, spans)
+            self.sweep(0, right, True, spans)
+
+    inside = [pl.ds(HALO // 2 + i * INNER, INNER) for i in range((cx + HALO) // INNER)]
     half = layers // 2
     fine, middle, column = (Level(n, refs) for n, refs in zip((layers, half, 1), levels))
     for level in (fine, middle, column):
         for p in range(2):
             for k in range(level.depth):
                 for t in both:
-                    level.seen[p, k, t, :, pl.ds(0, TOP), :] = jnp.zeros((2, TOP, cy), F32)
-                    level.seen[p, k, t, :, pl.ds(TOP + tall, TOP), :] = jnp.zeros((2, TOP, cy), F32)
+                    level.seen[p, k, t, :, 0:TOP + HALO] = jnp.zeros((2, TOP + HALO, cy), F32)
+                    level.seen[p, k, t, :, TOP + HALO + cx:] = jnp.zeros((2, TOP + HALO, cy), F32)
 
     def rows_of(ref, at):
         return lambda start: ref.at[at + (pl.ds(start, HALO),)]
@@ -522,7 +533,6 @@
         lax.fori_loop(0, 4, step, 0)
 
     block_row = lax.broadcasted_iota(jnp.int32, (count, cy), 0)
-    coarse_lane = lax.broadcasted_iota(jnp.int32, (count, cy), 1)
     shifts = (ny, count - ny, 1, count - 1)
 
     def coarse_begin(j, right, x):
@@ -549,24 +559,31 @@
             coarse_tab[6] = COARSE_WEIGHT / coarse_tab[0]
         wait()
         came = gathers[0][1][lax.rem(j, 2), :, 2, :]
-        right = came
-        for d in range(4):
-            right = right + pltpu.roll(pltpu.roll(came, shifts[d], 0), cy - 2 - 2 * d, 1)
+        moved = [pltpu.roll(came, shifts[d], 0) for d in range(4)]
+        right = []
+        for v in range(2):
+            part = came if v == 0 else pltpu.roll(came, cy - v, 1)
+            for d in range(4):
+                part = part + pltpu.roll(moved[d], cy - 2 - 2 * d - v, 1)
+            right.append(part)
         diag, crossed, east, west, north, south, weight = (coarse_tab[i] for i in range(7))
-        answer = right * weight
+        answer = [part * weight for part in right]
         for _ in range(CSWEEPS - 1):
-            other = jnp.where(coarse_lane % 2 == 0, pltpu.roll(answer, cy - 1, 1), pltpu.roll(answer, 1, 1))
-            applied = diag * answer + crossed * other - (
-                east * pltpu.roll(answer, count - ny, 0) + west * pltpu.roll(answer, ny, 0)
-                + north * pltpu.roll(answer, count - 1, 0) + south * pltpu.roll(answer, 1, 0))
-            answer = answer + (right - applied) * weight
+            old = answer
+            answer = []
+            for v in range(2):
+                applied = diag * old[v] + crossed * old[1 - v] - (
+                    east * pltpu.roll(old[v], count - ny, 0) + west * pltpu.roll(old[v], ny, 0)
+                    + north * pltpu.roll(old[v], count - 1, 0) + south * pltpu.roll(old[v], 1, 0))
+                answer.append(old[v] + (right[v] - applied) * weight)
         hops = ((0, 0),) + STEPS[:4]
         known = {}
 
         def value(dx, dy):
             if (dx, dy) not in known:
-                line = jnp.sum(jnp.where(block_row == me + dx * ny + dy, answer, 0.0), axis=0, keepdims=True)
-                known[dx, dy] = jnp.concatenate([line[:, 0:1], line[:, 1:2]], axis=0)
+                here = block_row == me + dx * ny + dy
+                known[dx, dy] = jnp.concatenate(
+                    [jnp.sum(jnp.where(here, part, 0.0), axis=0, keepdims=True)[:, 0:1] for part in answer], axis=0)
             return known[dx, dy]
 
         found = []
@@ -579,6 +596,21 @@
             found.append(out)
         return found
 
+    def build_lifts():
+        for t in both:
+            for out, source in ((lift_side, lambda k: middle.side[k, t]), (lift_cross, lambda k: middle.cross[t] if k == 0 else 0.0)):
+                last = 0.0
+                for k in range(half):
+                    value = source(k)
+                    if k > 0:
+                        value = value + middle.vert[k - 1, t] * last
+                    last = value * middle.inverse[k, t]
+                    out[k, t] = last
+                out[half - 1, t] = LINE_WEIGHT * last
+                for k in reversed(range(half - 1)):
+                    last = out[k, t] - middle.upper[k, t] * last
+                    out[k, t] = LINE_WEIGHT * last
+
     def swapped(x):
         return jnp.concatenate([x[1:2], x[0:1]], axis=0)
 
@@ -592,7 +624,7 @@
     def point_apply(xs):
         return point_cross[...] * swapped(xs[0]) + apply_tables(big, xs)
 
-    def point_cycle(j, right):
+    def point_cycle(j, right, merge):
         x_out[0] = right * (POINT_WEIGHT / point_diag[...])
         swap = near_swap(0, 0)
         swap.start()
@@ -606,12 +638,13 @@
         packer.finish()
         swap_side.start()
         pl.when(j == 0)(build_near)
+        pl.when(j == 0)(build_lifts)
         scale = POINT_WEIGHT / point_diag[...]
         swap.wait()
         first = [right * scale] + [x_in[0, BACK[d]] for d in range(4)]
         x = first[0] + (right - point_apply(first)) * scale
         coarse_wait = coarse_begin(j, right, x)
-        merge_side()
+        merge()
         found = coarse_end(j, coarse_wait)
         hops = ((0, 0),) + STEPS[:4]
 
@@ -630,20 +663,30 @@
             xs.append(local[0] + first[i] - moved + found[i])
         return xs[0] + (right - point_apply(xs)) * scale
 
-    def merge_side():
+    def mid_put(k, v):
+        def put(value):
+            middle.field[0, k, 1, v] = value
+            middle.seen[0, k, 1, v, TOP:TOP + tall] = value * ice_ext[1]
+        return put
+
+    whole = pl.ds(0, tall)
+
+    def merge_side(right0, right1):
         swap_side.wait()
         column.field[0, 0, 0] = jnp.concatenate([col_rows[0, 0], column.field[1, 0, 0, :, own], col_rows[1, 0]], axis=1)
         for e in range(2):
             column.right[0, 0, :, ends(e)] = col_rows[e, 1]
         for k in range(half):
-            middle.field[0, k, 0] = jnp.concatenate([mid_rows[0, k], middle.field[1, k, 0, :, own], mid_rows[1, k]],
-                                                    axis=1)
+            middle.put(0, k, 0, whole, jnp.concatenate(
+                [mid_rows[0, k], middle.field[1, k, 0, :, own], mid_rows[1, k]], axis=1))
         puts = []
         for v in range(2):
             puts += [put_to(column.field, 0, 0, 1, v), put_to(column.right, 0, 1, v)]
         for k in range(half):
-            puts += [put_to(middle.field, 0, k, 1, v) for v in range(2)]
+            puts += [mid_put(k, v) for v in range(2)]
         unpack(side_land, puts)
+        middle.sweep(0, right1, spans=inside, plain=True)
+        fine.sweep(1, right0, spans=inside, plain=True)
 
     def spread_points(x):
         far_out[...] = x
@@ -688,33 +731,49 @@
         swap_right(j).wait()
         unpack(right_land, [put_to(basis, j, v, k, 1) for k in range(layers) for v in range(2)])
         fine.before(right0)
-        fine.leftover(1, right0, collect(middle, 2))
-        middle.before(right1)
-        middle.leftover(1, right1, collect(column, half))
-        column.before(right2)
+        fine.leftover(1, right0, collect(middle, 2), spans=inside)
+        middle.before(right1, inside)
+        middle.leftover(1, right1, collect(column, half), spans=inside)
+        column.before(right2, inside)
         kept = []
         column.leftover(1, right2, lambda k, t, here, value: kept.append(value), (0,), (own,))
-        found = spread_points(point_cycle(j, restrict_points(kept[0][0], kept[0][1])))
-
-        whole = pl.ds(0, tall)
+        found = spread_points(point_cycle(j, restrict_points(kept[0][0], kept[0][1]),
+                                          lambda: merge_side(right0, right1)))
+
         for t in both:
             column.put(0, 0, t, whole, found[t] + column.field[0, 0, t])
-        column.after(right2)
-        for k in range(half):
+        column.sweep(0, right2)
+        column.sweep(1, right2)
+        for here in inside:
+            outs = column.sums(0, 0, here, both)[1]
             for t in both:
-                middle.put(0, k, t, whole, column.field[0, 0, t] + middle.field[0, k, t])
-        middle.after(right1)
-        for k in range(layers):
-            for t in both:
-                fine.put(0, k, t, whole, fine.field[1, k, t] + middle.field[0, k // 2, t])
-        fine.after(right0, [pl.ds(HALO // 2 + i * 8, 8) for i in range(cx // 8 + 1)])
+                value = column.field[0, 0, t, :, here]
+                part = (1.0 - LINE_WEIGHT) * value
+                other = jnp.stack([value[1], value[0]])
+                for k in range(half):
+                    middle.put(0, k, t, here, (middle.field[1, k, t, :, here] + part)
+                               + (lift_side[k, t, here][None] * outs[t] - lift_cross[k, t, here][None] * other))
+        middle.sweep(0, right1, spans=inside)
+        held = []
+
+        def lifted(k, here):
+            if k % 2 == 0:
+                held[:] = middle.sums(1, k // 2, here, both)
+            return fine.sideways(k, here, both, *held)
+
+        def lift(k, t, here, value):
+            fine.put(1, k, t, here, (fine.field[0, k, t, :, here] + value)
+                     + (1.0 - LINE_WEIGHT) * middle.field[1, k // 2, t, :, here])
+
+        fine.solve(lifted, lift, inside)
+        fine.sweep(1, right0, spans=inside)
 
         packer = Packer(right_pack)
 
         for k in range(layers):
             here = fine.field[0, k, 0, :, own]
             stored[j, :, k] = here
-            out = fine.sideways(0, k, own, (0,))[0] - fine.diag[k, 0, own][None] * here
+            out = fine.beside(0, k, own, (0,))[0] - fine.diag[k, 0, own][None] * here
             if k + 1 < layers:
                 out = out + fine.vert[k, 0, own][None] * fine.field[0, k + 1, 0, :, own]
             if k > 0:
@@ -761,8 +820,8 @@
             out = out + weights[j] * stored[j, :, k]
             rest = rest - weights[j] * (basis[j, :, k, 0, own] - basis[j + 1, :, k, 0, own])
         for v in range(2):
-            solution[pl.ds((v * layers + k) * cx, cx)] = out[v]
-            residual[pl.ds((v * layers + k) * cx, cx)] = rest[v]
+            result[pl.ds((v * layers + k) * cx, cx)] = out[v]
+            result[pl.ds((2 * layers + v * layers + k) * cx, cx)] = rest[v]
 
 
 def solution(mesh):
@@ -787,8 +846,8 @@
             )
 
         def swap(planes, pieces):
-            tiles = -(-planes * SLOT // cy)
-            return (vm(tiles, cx, cy), vm(2, tiles, tall, cy), dma((8, pieces)), dma((8, pieces)))
+            tiles = -(-planes * HALO // cy)
+            return (vm(2, tiles, cx, cy), vm(2, tiles, tall, cy), dma((8, pieces)), dma((8, pieces)))
 
         scratch = (
             (level(layers), level(half), level(1)),
@@ -804,24 +863,24 @@
             (vm(2, cy), vm(8, 2, cy), dma((8, 1)), dma((8, 1))),
             (vm(2, half, 2, HALO, cy), vm(2, 2, 2, HALO, cy)),
             (vm(24 + cx + cy, cy), vm(4, 24 + cx + cy, cy), vm(4, 5 * cy, 2 * cy, dtype=BF16), dma((4, 1)), dma((4, 1))),
-            vm(7, count, cy),
+            vm(7, count, cy), vm(half, 2, tall, cy), vm(half, 2, tall, cy),
         )
         flat, tree = jax.tree.flatten(scratch)
 
         def run(*refs):
-            kernel(nx, ny, layers, cx, cy, *refs[:9], *jax.tree.unflatten(tree, refs[9:]))
-
-        shape = jax.ShapeDtypeStruct((2 * layers * cx, cy), F32)
+            kernel(nx, ny, layers, cx, cy, *refs[:8], *jax.tree.unflatten(tree, refs[8:]))
+
+        shape = jax.ShapeDtypeStruct((4 * layers * cx, cy), F32)
         whole = pl.BlockSpec(memory_space=pltpu.VMEM)
         outs = pl.pallas_call(
             run,
-            out_shape=(shape, shape),
+            out_shape=shape,
             in_specs=[whole] * 7,
-            out_specs=(whole, whole),
+            out_specs=whole,
             scratch_shapes=flat,
             compiler_params=pltpu.CompilerParams(has_side_effects=True, vmem_limit_bytes=60 * 1024 * 1024),
         )(forcing, viscosity, spread, coupling, friction, mask, aggs)
-        return tuple(out.reshape(forcing.shape) for out in outs)
+        return tuple(out.reshape(forcing.shape) for out in jnp.split(outs, 2))
 
     return jax.shard_map(
         body,

time: 101 us -> 91.4 us (0.905)
  Pallas kernels: 97.7 us -> 88.6 us
    pallas_call x1, Pallas kernels: 97.7 us -> 88.6 us  [body(): pl.pallas_call(run, out_shape=shape, in_specs=[whole] * 7, out_specs=whol...]
    unnamed x4 -> x0, local copies, waits for them, and re-layouts: 2.49 us -> none
    split x0 -> x1, local copies, waits for them, and re-layouts: none -> 1.95 us  [body(): return tuple((out.reshape(forcing.shape) for out in jnp.split(outs, 2)))]
where the time goes in v3:
time: 91.4 us; the launch traced here: 91.2 us
  Pallas kernels  88.6 us (97%)
  local copies, waits for them, and re-layouts  1.95 us (2%)
    pallas_call x1, Pallas kernels, body(): pl.pallas_call(run, out_shape=shape, in_specs=[whole] * 7, out_specs=whol...  88.6 us
    split x1, local copies, waits for them, and re-layouts, body(): return tuple((out.reshape(forcing.shape) for out in jnp.split(outs, 2)))  1.95 us

profile of v3, /device:TPU:0, one launch (start us, length us, event | category | flops | bytes accessed | tf_op | source)
XLA Modules:
  0.0 91.2 jit_solution(9236524424715272512)
XLA Ops:
  0.6 88.6 %shard_map.86 = f32[1280,128]{1,0:T(8,128)} custom-call(f32[2,20,16,128]{3,2,1,0:T(8,128)} %refs_0_.1, f32[20,16,128]{2,1,0:T(8,128)} %refs_1_.1, f32[20,16,128]{2,1,0:T(8,128)} %refs_2_.1, f32[16,128]{1,0:T(8,128)} %refs_3_.1, f32[16,128]{1,0:T(8,128)} %refs_4_.1, s32[16,128]{1,0:T(8,128)} %refs_5_.1, s32[16,128]{1,0:T(8,128)} %refs_6_.1), custom_call_target="tpu_custom_call" | custom-call | tf_op jit(solution)/shard_map/pallas_call | solution.py:875
  89.3 1.9 %fusion = (f32[640,128]{1,0:T(8,128)}, f32[640,128]{1,0:T(8,128)}) fusion(f32[1280,128]{1,0:T(8,128)} %shard_map.86), kind=kLoop, calls=%fused_computation | loop fusion | bytes 1310720 | tf_op jit(solution)/shard_map/split | solution.py:883

commit v4 on v3

--- a/solution.py
+++ b/solution.py
@@ -15,6 +15,7 @@
 BF16 = jnp.bfloat16
 TOP = 8
 HALO = 8
+REACH = 6
 CHUNK = 16
 INNER = 8
 STEPS = ((1, 0), (-1, 0), (0, 1), (0, -1), (1, 1), (1, -1), (-1, 1), (-1, -1))
@@ -50,13 +51,12 @@
      (mid_rows, col_rows), (near_out, near_in, big_near, near_send, near_recv),
      coarse_tab, lift_side, lift_cross) = scratch
     tall = cx + 2 * HALO
+    half = layers // 2
     own = pl.ds(HALO, cx)
-    slots = cy // HALO
     lane = lax.broadcasted_iota(jnp.int32, (cx, cy), 1)
     row = lax.broadcasted_iota(jnp.int32, (cx, cy), 0)
     first_lane, last_lane = lane == 0, lane == cy - 1
     long_lane = lax.broadcasted_iota(jnp.int32, (tall, cy), 1)
-    kept_lane = (long_lane < HALO) | (long_lane >= cy - HALO)
 
     exists, peers = [], []
     for dx, dy in STEPS:
@@ -99,9 +99,9 @@
                     for _, ref in self.pieces[BACK[d]]:
                         ref[...] = jnp.zeros(ref.shape, F32)
 
-    def edges(rows, packed, landed):
-        low, high = pl.ds(0, HALO), pl.ds(cx - HALO, HALO)
-        top, bottom = pl.ds(0, HALO), pl.ds(HALO + cx, HALO)
+    def edges(rows, packed, landed, reach=HALO):
+        low, high = pl.ds(0, reach), pl.ds(cx - reach, reach)
+        top, bottom = pl.ds(HALO - reach, reach), pl.ds(HALO + cx, reach)
         return [
             [(src(cx - HALO), dst(0)) for src, dst in rows],
             [(src(0), dst(1)) for src, dst in rows],
@@ -116,19 +116,29 @@
     def ends(e):
         return pl.ds(0, HALO) if e == 0 else pl.ds(HALO + cx, HALO)
 
+    def slots_of(width):
+        return cy // width if cy % width == 0 else (cy - width) // width // 2 * 2
+
     class Packer:
-        def __init__(self, out):
+        def __init__(self, out, width=HALO):
             self.out = out
+            self.width = width
+            self.slots = slots_of(width)
             self.at = 0
             self.tiles = None
 
         def add(self, value):
-            s, m = divmod(self.at, slots)
-            moved = pltpu.roll(value, (HALO * m + HALO) % cy, 1)
-            self.tiles = [moved] * 2 if m == 0 else [
-                jnp.where(lane // HALO == (m + i) % slots, moved, self.tiles[i]) for i in range(2)]
+            s, m = divmod(self.at, self.slots)
+            w = self.width
+            moved = pltpu.roll(value, (w * m + w) % cy, 1)
+            if m == 0:
+                self.tiles = [moved] * 2
+            else:
+                for i in range(2):
+                    low = (m + i) * w % cy
+                    self.tiles[i] = jnp.where((lane >= low) & (lane < low + w), moved, self.tiles[i])
             self.at += 1
-            if m == slots - 1:
+            if m == self.slots - 1:
                 self.flush(s)
 
         def flush(self, s):
@@ -138,16 +148,18 @@
 
         def finish(self):
             if self.tiles is not None:
-                self.flush((self.at - 1) // slots)
-
-    def unpack(landed, puts):
-        south = long_lane // HALO % 2 == 0
+                self.flush((self.at - 1) // self.slots)
+
+    def unpack(landed, puts, w=HALO):
+        south = long_lane // w % 2 == 0
+        kept = (long_lane < w) | (long_lane >= cy - w)
+        slots = slots_of(w)
         comb = None
         for i, put in enumerate(puts):
             s, m = divmod(i, slots)
             if m == 0:
                 comb = [jnp.where(south, landed[e, s], landed[1 - e, s]) for e in range(2)]
-            put(jnp.where(kept_lane, pltpu.roll(comb[m % 2], (2 * cy - HALO * m - HALO) % cy, 1), 0.0))
+            put(jnp.where(kept, pltpu.roll(comb[m % 2], (2 * cy - w * m - w) % cy, 1), 0.0))
 
     chunks = [pl.ds(i * CHUNK, CHUNK) for i in range(tall // CHUNK)]
     both = (0, 1)
@@ -248,7 +260,6 @@
             self.sweep(0, right, True, spans)
 
     inside = [pl.ds(HALO // 2 + i * INNER, INNER) for i in range((cx + HALO) // INNER)]
-    half = layers // 2
     fine, middle, column = (Level(n, refs) for n, refs in zip((layers, half, 1), levels))
     for level in (fine, middle, column):
         for p in range(2):
@@ -257,23 +268,30 @@
                     level.seen[p, k, t, :, 0:TOP + HALO] = jnp.zeros((2, TOP + HALO, cy), F32)
                     level.seen[p, k, t, :, TOP + HALO + cx:] = jnp.zeros((2, TOP + HALO, cy), F32)
 
-    def rows_of(ref, at):
-        return lambda start: ref.at[at + (pl.ds(start, HALO),)]
-
-    any_k = slice(None)
+    def tail(lo, offset):
+        return pl.ds(offset + lo + (HALO - REACH if lo else 0), REACH)
+
+    def near_ends(e):
+        return pl.ds(HALO - REACH if e == 0 else HALO + cx, REACH)
 
     (first_pack, first_land, first_send, first_recv) = first_swap
     swap0 = Swap(edges([
-        (lambda lo: viscosity.at[:, pl.ds(lo, HALO)], lambda e: visc.at[:, 0, ends(e)]),
-        (lambda lo: spread.at[:, pl.ds(lo, HALO)], lambda e: spr.at[:, 0, ends(e)]),
+        (lambda lo: viscosity.at[:, tail(lo, 0)], lambda e: visc.at[:, 0, near_ends(e)]),
+        (lambda lo: spread.at[:, tail(lo, 0)], lambda e: spr.at[:, 0, near_ends(e)]),
         (lambda lo: misc.at[:, 0, pl.ds(HALO + lo, HALO)], lambda e: misc.at[:, 0, ends(e)]),
     ], first_pack, first_land), first_send, first_recv)
     (right_pack, right_land, right_send, right_recv) = right_swap
 
+    side_tiles = right_pack.shape[1] // 2
+
     def swap_right(j):
-        return Swap(edges([(lambda lo: basis.at[j, :, :, 0, pl.ds(HALO + lo + (2 if lo else 0), HALO - 2)],
-                            lambda e: basis.at[j, :, :, 0, pl.ds(2 if e == 0 else HALO + cx, HALO - 2)])],
-                          right_pack, right_land), right_send, right_recv)
+        def part(h):
+            span, tiles = pl.ds(h * half, half), pl.ds(h * side_tiles, side_tiles)
+            return Swap(edges([(lambda lo: basis.at[j, :, span, 0, tail(lo, HALO)],
+                                lambda e: basis.at[j, :, span, 0, near_ends(e)])],
+                              right_pack.at[:, tiles], right_land.at[:, tiles], REACH),
+                        right_send.at[h], right_recv.at[h])
+        return [part(h) for h in range(2)]
 
     (side_pack, side_land, side_send, side_recv) = side_swap
     swap_side = Swap(edges([
@@ -302,18 +320,29 @@
         packer.add(spread[k])
     packer.finish()
     swap0.start(range(2, 8))
-    packer = Packer(right_pack)
+    for h in range(2):
+        packer = Packer(right_pack.at[:, pl.ds(h * side_tiles, side_tiles)], REACH)
+        for k in range(h * half, h * half + half):
+            basis[0, :, k, 0, own] = forcing[:, k]
+            for v in range(2):
+                packer.add(forcing[v, k])
+        packer.finish()
+    for part in swap_right(0):
+        part.start()
+    for j in range(ITERS):
+        for part in swap_right(j):
+            part.clear()
+        for k in range(layers):
+            basis[j, :, k, 0, 0:HALO - REACH] = jnp.zeros((2, HALO - REACH, cy), F32)
+            basis[j, :, k, 0, HALO + cx + REACH:tall] = jnp.zeros((2, HALO - REACH, cy), F32)
     for k in range(layers):
-        basis[0, :, k, 0, own] = forcing[:, k]
-        for v in range(2):
-            packer.add(forcing[v, k])
-    packer.finish()
-    swap_right(0).start()
-    for j in range(ITERS):
-        swap_right(j).clear()
-        for k in range(layers):
-            basis[j, :, k, 0, 0:HALO - 6] = jnp.zeros((2, HALO - 6, cy), F32)
-            basis[j, :, k, 0, tall - HALO + 6:tall] = jnp.zeros((2, HALO - 6, cy), F32)
+        for ref in (visc, spr):
+            ref[k, 0, 0:HALO - REACH] = jnp.zeros((HALO - REACH, cy), F32)
+            ref[k, 0, HALO + cx + REACH:tall] = jnp.zeros((HALO - REACH, cy), F32)
+    for e in range(2):
+        for n in range(right_land.shape[1]):
+            right_land[e, n, 0:HALO - REACH] = jnp.zeros((HALO - REACH, cy), F32)
+            right_land[e, n, HALO + cx + REACH:tall] = jnp.zeros((HALO - REACH, cy), F32)
     swap0.clear()
     swap_side.clear()
     swap_far.clear()
@@ -728,8 +757,10 @@
                     coarser.right[k // size, t, :, here] = held[t]
             return emit
 
-        swap_right(j).wait()
-        unpack(right_land, [put_to(basis, j, v, k, 1) for k in range(layers) for v in range(2)])
+        for h, part in enumerate(swap_right(j)):
+            part.wait()
+            unpack(right_land.at[:, pl.ds(h * side_tiles, side_tiles)],
+                   [put_to(basis, j, v, h * half + k, 1) for k in range(half) for v in range(2)], REACH)
         fine.before(right0)
         fine.leftover(1, right0, collect(middle, 2), spans=inside)
         middle.before(right1, inside)
@@ -768,8 +799,8 @@
         fine.solve(lifted, lift, inside)
         fine.sweep(1, right0, spans=inside)
 
-        packer = Packer(right_pack)
-
+        packer = Packer(right_pack, REACH)
+        parts = swap_right(j + 1)
         for k in range(layers):
             here = fine.field[0, k, 0, :, own]
             stored[j, :, k] = here
@@ -782,11 +813,10 @@
             basis[j + 1, :, k, 0, own] = value
             for v in range(2):
                 packer.add(value[v])
-        packer.finish()
-
-        @pl.when(j < ITERS - 1)
-        def _():
-            swap_right(j + 1).start()
+            if k % half == half - 1:
+                packer.finish()
+                packer = Packer(right_pack.at[:, pl.ds(side_tiles, side_tiles)], REACH)
+                pl.when(j < ITERS - 1)(parts[k // half].start)
         return carry
 
     lax.fori_loop(0, ITERS, iteration, 0)
@@ -845,9 +875,13 @@
                 vm(n, 2, 2, tall, cy),
             )
 
-        def swap(planes, pieces):
-            tiles = -(-planes * HALO // cy)
+        def swap(planes, pieces, slots=cy // HALO):
+            tiles = -(-planes // slots)
             return (vm(2, tiles, cx, cy), vm(2, tiles, tall, cy), dma((8, pieces)), dma((8, pieces)))
+
+        def wide_swap(planes, slots):
+            tiles = -(-planes // slots) * 2
+            return (vm(2, tiles, cx, cy), vm(2, tiles, tall, cy), dma((2, 8, 1)), dma((2, 8, 1)))
 
         scratch = (
             (level(layers), level(half), level(1)),
@@ -858,7 +892,7 @@
             (vm(2, 2, cy), vm(2, 4, 2, cy), dma((2, 4, 1)), dma((2, 4, 1))),
             tuple((vm(n, cy), vm(2, count, n, cy), dma(()), dma((2,))) for n in (3, 1, 8)),
             swap(4 + 2 * layers, 3),
-            swap(2 * layers, 1),
+            wide_swap(2 * half, (cy - REACH) // REACH // 2 * 2),
             swap(4 + 2 * half, 3),
             (vm(2, cy), vm(8, 2, cy), dma((8, 1)), dma((8, 1))),
             (vm(2, half, 2, HALO, cy), vm(2, 2, 2, HALO, cy)),

time: 91.4 us -> 88.4 us (0.967)
  Pallas kernels: 88.6 us -> 85.6 us
    pallas_call x1, Pallas kernels: 88.6 us -> 85.6 us  [body(): pl.pallas_call(run, out_shape=shape, in_specs=[whole] * 7, out_specs=whol...]
where the time goes in v4:
time: 88.4 us; the launch traced here: 88.2 us
  Pallas kernels  85.6 us (97%)
  local copies, waits for them, and re-layouts  1.95 us (2%)
    pallas_call x1, Pallas kernels, body(): pl.pallas_call(run, out_shape=shape, in_specs=[whole] * 7, out_specs=whol...  85.6 us
    split x1, local copies, waits for them, and re-layouts, body(): return tuple((out.reshape(forcing.shape) for out in jnp.split(outs, 2)))  1.95 us

profile of v4, /device:TPU:0, one launch (start us, length us, event | category | flops | bytes accessed | tf_op | source)
XLA Modules:
  0.0 88.2 jit_solution(9413964683277437900)
XLA Ops:
  0.6 85.6 %shard_map.86 = f32[1280,128]{1,0:T(8,128)} custom-call(f32[2,20,16,128]{3,2,1,0:T(8,128)} %refs_0_.1, f32[20,16,128]{2,1,0:T(8,128)} %refs_1_.1, f32[20,16,128]{2,1,0:T(8,128)} %refs_2_.1, f32[16,128]{1,0:T(8,128)} %refs_3_.1, f32[16,128]{1,0:T(8,128)} %refs_4_.1, s32[16,128]{1,0:T(8,128)} %refs_5_.1, s32[16,128]{1,0:T(8,128)} %refs_6_.1), custom_call_target="tpu_custom_call" | custom-call | tf_op jit(solution)/shard_map/pallas_call | solution.py:909
  86.3 1.9 %fusion = (f32[640,128]{1,0:T(8,128)}, f32[640,128]{1,0:T(8,128)}) fusion(f32[1280,128]{1,0:T(8,128)} %shard_map.86), kind=kLoop, calls=%fused_computation | loop fusion | bytes 1310720 | tf_op jit(solution)/shard_map/split | solution.py:917
